TPU v7x, 128 devices: a whole 4x4x4 slice. The times are simulated.
128 devices in a mesh: field: 2 (over core), dom: 64 (over x, y, z).
Axes of the slice: x: 4, y: 4, z: 4, core: 2. Of those that a mesh axis runs over, the one named last changes fastest.
Arguments:
- modes: float32 [2, 40, 524288], P('field', None, 'dom'), may hold values from -6 to 6
- previous: float32 [2, 40, 524288], P('field', None, 'dom'), may hold values from -6 to 6
- kinds: int32 [2, 3, 1024], P('field'), may hold values from 0 to 3
- scales: float32 [2, 3, 1024], P('field'), may hold values from 0.5 to 4
- tables: bfloat16 [2, 3, 4, 512, 512], P('field'), may hold values from -2 to 6, as said below
- wet_rows: int32 [2, 196608], P('field', 'dom'), may hold values from 0 to 8191, as said below
- wet_counts: int32 [64], P('dom'), may hold values from 768 to 3072, as said below
- coupling: float32 [196608], P('dom'), may hold values from -6 to 6
Outputs:
- basis: float32 [2, 120, 524288], P('field', None, 'dom')
- projected: float32 [120, 120], replicated
Inputs may be any that keep to these rules, and one draw needn't show every extreme that they name: `tables`: tables of offset 0 are symmetric. `wet_rows`: within each subdomain and field the 3072 row numbers are distinct. `wet_counts`: some subdomain uses all 3072 slots.
All inputs are finite; a program needn't handle non-finite values.
Results may differ from a plain program's by a relative error of at most 0.00045.
The roundings to bfloat16 on the way count: a program that leaves them out, or rounds other values in their place, can miss the bound.
Values may be sent and summed in bfloat16 or wider, within the bound.
No kernel may reach another device: no remote copies, remote signals or barrier semaphores. Data moves between devices by JAX's collectives and lax.ppermute only.
A program may use at most 192 MiB of HBM per device.

v0:
```python
import jax
import jax.numpy as jnp
from jax import lax
from jax.experimental import pallas as pl
from jax.experimental.pallas import tpu as pltpu
from jax.sharding import Mesh
from jax.sharding import PartitionSpec as P


BS = 512
NTYPE = 4
NBR = 16
NBLK = 1024
ROWS = NBR * BS
HALO = 2 * BS
MODES = 40
IFACE = 3072
LANES = 128
TILES = ROWS // LANES
DOM = ("dom_0", "dom_1", "dom_2")
FIELD_DOM = ("field", "dom_0", "dom_1", "dom_2")
ALL_DEV = 128
F32 = jnp.float32
BF16 = jnp.bfloat16

VMEM = pl.BlockSpec(memory_space=pltpu.VMEM)
SMEM = pl.BlockSpec(memory_space=pltpu.SMEM)
HBM = pl.BlockSpec(memory_space=pltpu.HBM)
PAIR = 2 * MODES
SINGLE = 48
UNROLL = 2
SLOTS = IFACE // NBR
WIDTH = 1024

OPS = ((0, 0, 0, 0), (1, -1, -1, 0), (2, -2, -2, 0), (1, 1, 0, 1), (2, 2, 0, 1))


def params(mib):
    return pltpu.CompilerParams(vmem_limit_bytes=mib << 20)


def shape(*dims, kind=F32):
    return jax.ShapeDtypeStruct(dims, kind)


def domain_index():
    return (lax.axis_index(DOM[0]) * 4 + lax.axis_index(DOM[1])) * 4 + lax.axis_index(DOM[2])


def in_hbm(value):
    return pltpu.with_memory_space_constraint(value, pltpu.HBM)


def swap_field(value):
    return lax.ppermute(value, "field", [(0, 1), (1, 0)])


def from_left(value):
    return lax.ppermute(value, DOM, [(i, i + 1) for i in range(63)])


def from_right(value):
    return lax.ppermute(value, DOM, [(i + 1, i) for i in range(63)])


def exchange(rows):
    return lax.all_to_all(rows, FIELD_DOM, 0, 0, tiled=True)


def round_kernel(
    modes, prev, coupling, rows, counts,
    modes_v, prev_v, whole, head, tail, weights, rows_v, sems,
):
    pairs = ((modes, modes_v), (prev, prev_v), (coupling, weights), (rows, rows_v))
    loads = [
        pltpu.make_async_copy(source, target, sems.at[index])
        for index, (source, target) in enumerate(pairs)
    ]
    for load in loads:
        load.start()
    slot = lax.broadcasted_iota(jnp.int32, weights.shape, 0) * LANES + lax.broadcasted_iota(
        jnp.int32, weights.shape, 1
    )
    for load in loads:
        load.wait()
    weights[...] = jnp.where(slot < counts[0], weights[...], 0.0)
    rounded = jnp.concatenate([modes_v[...], prev_v[...]], axis=0).astype(BF16)
    whole[...] = rounded
    head[...] = rounded[:, :HALO]
    tail[...] = rounded[:, ROWS - HALO :]


def rounded_parts(modes, prev, coupling, rows, counts):
    plane = shape(MODES, ROWS)
    end = shape(PAIR, HALO, kind=BF16)
    slots = shape(IFACE // LANES, LANES)
    return pl.pallas_call(
        round_kernel,
        out_shape=(plane, plane, shape(PAIR, ROWS, kind=BF16), end, end, slots,
                   shape(IFACE // LANES, LANES, kind=jnp.int32)),
        in_specs=[HBM] * 4 + [SMEM],
        out_specs=[VMEM] * 7,
        scratch_shapes=[pltpu.SemaphoreType.DMA((4,))],
        compiler_params=params(12),
        name="rounded",
    )(
        *map(in_hbm, (modes, prev, coupling.reshape(slots.shape), rows.reshape(slots.shape))),
        counts,
    )


def block_sum(b, at, blocks, tables, flipped, kinds, scales, beside=None):
    first = domain_index() * NBR
    total = None
    for index, (offset, shift, owner, flip) in enumerate(OPS):
        block = offset * NBLK + jnp.maximum(first + b + owner, 0)
        kind = kinds[block]
        if flip:
            table = flipped[(offset - 1) * NTYPE + kind]
        else:
            table = tables[offset * NTYPE + kind]
        product = jnp.dot(blocks[at + shift], table, preferred_element_type=F32)
        if beside is not None:
            beside(index, product[0, 0])
        product = scales[block] * product
        total = product if total is None else total + product
    return total


def coupler(base, total, dots, rows, rows_o, weights, other_t, coup):
    share = total // dots
    taken = []

    def beside(_, value):
        if len(taken) == dots:
            return
        late = jnp.where(value == value, 0, 1)
        start = jnp.minimum(base + len(taken) * share + late, IFACE - share)
        taken.append(start)
        for v in range(share):
            slot = start + v
            coup[pl.ds(rows[slot], 1), :] = other_t[pl.ds(rows_o[slot], 1), :] * weights[slot]

    return beside


def inner_kernel(
    modes, prev, other, tables_in, kinds, scales, rows, rows_o, weights,
    partial_x, partial_p, coup, tables, flipped, blocks, other_t, sem,
):
    load = pltpu.make_async_copy(tables_in, tables, sem)
    load.start()
    for b in range(NBR):
        span = slice(b * BS, (b + 1) * BS)
        blocks[b] = jnp.concatenate([modes[:, span], prev[:, span]], axis=0).astype(BF16)
    for c in range(TILES):
        span = slice(c * LANES, (c + 1) * LANES)
        other_t[span, :PAIR] = other[:, span].astype(F32).T
    coup[...] = jnp.zeros_like(coup)
    load.wait()
    for index in range(2 * NTYPE):
        flipped[index] = tables[NTYPE + index].T
    steps = (NBR - 4) // UNROLL
    slots = IFACE // steps

    def step(index, carry):
        beside = coupler(index * slots, slots, 8, rows, rows_o, weights, other_t, coup)
        for u in range(UNROLL):
            b = 2 + index * UNROLL + u
            total = block_sum(b, b, blocks, tables, flipped, kinds, scales, beside)
            span = pl.ds(pl.multiple_of(b * BS, BS), BS)
            partial_x[:, span] = total[:MODES]
            partial_p[:, span] = total[MODES:]
        return carry

    lax.fori_loop(0, steps, step, 0)


def outer_kernel(
    modes, prev, left, right, partial_x, partial_p, coup, tables, flipped, kinds, scales,
    image_x, image_p, ratios, head, tail, sums, ends,
):
    first = domain_index() * NBR
    for b in range(2):
        span = slice(b * BS, (b + 1) * BS)
        ends[b] = left[:, span]
        ends[10 + b] = right[:, span]
    for at, b in ((2, 0), (3, 1), (4, 2), (5, 3), (6, 12), (7, 13), (8, 14), (9, 15)):
        span = slice(b * BS, (b + 1) * BS)
        ends[at] = jnp.concatenate([modes[:, span], prev[:, span]], axis=0).astype(BF16)

    def step(index, carry):
        for u in range(2):
            b = index * (NBR - 2) + u
            total = block_sum(b, 2 + index * 6 + u, ends, tables, flipped, kinds, scales)
            span = pl.ds(pl.multiple_of(b * BS, BS), BS)
            partial_x[:, span] = total[:MODES]
            partial_p[:, span] = total[MODES:]
        return carry

    lax.fori_loop(0, 2, step, 0)
    on_diagonal = lax.broadcasted_iota(jnp.int32, (LANES, LANES), 0) == lax.broadcasted_iota(
        jnp.int32, (LANES, LANES), 1
    )
    lines = []
    for part in range(BS // LANES):
        span = slice(part * LANES, (part + 1) * LANES)
        lines.append(
            [
                jnp.sum(
                    jnp.where(on_diagonal, tables[kind, span, span].astype(F32), 0.0),
                    axis=0, keepdims=True,
                )
                for kind in range(NTYPE)
            ]
        )
    squares = jnp.zeros((MODES, LANES), F32)
    crossed = jnp.zeros((MODES, LANES), F32)
    for c in range(TILES):
        b, part = divmod(c, BS // LANES)
        span = slice(c * LANES, (c + 1) * LANES)
        coupled = coup[span, :].T
        value = partial_x[:, span] + coupled[:MODES]
        image_x[:, span] = value
        image_p[:, span] = partial_p[:, span] + coupled[MODES:PAIR]
        own = modes[:, span]
        squares += own * own
        crossed += own * value
        kind = kinds[first + b]
        line = lines[part][0]
        for other_kind in range(1, NTYPE):
            line = jnp.where(kind == other_kind, lines[part][other_kind], line)
        inverse = 1.0 / (scales[first + b] * line)
        ratio = jnp.concatenate([value * inverse, own * inverse], axis=0)
        ratios[:, span] = ratio
        if c < HALO // LANES:
            head[:, span] = ratio
        if c >= TILES - HALO // LANES:
            at = (c - (TILES - HALO // LANES)) * LANES
            tail[:, at : at + LANES] = ratio
    both = jnp.concatenate([squares, crossed, jnp.zeros((LANES - PAIR, LANES), F32)], axis=0)
    total = jnp.sum(both.T, axis=0, keepdims=True)
    sums[...] = jnp.broadcast_to(total, (ALL_DEV, LANES))


def second_kernel(
    gathered, ratios, left, right, other, tables, kinds, scales, rows, rows_o, weights,
    flipped, modes, prev, image_x, image_p, residual_out, packed,
    blocks, other_t, coup, image_r, gram, residual, sem,
):
    total = jnp.sum(gathered[...], axis=0, keepdims=True)
    column = jnp.broadcast_to(total, (LANES, LANES)).T
    quotient = column[MODES:PAIR, :] / column[:MODES, :]

    def residual_of(source, span):
        return source[:MODES, span] - source[MODES:, span] * quotient

    for c in range(HALO // LANES):
        span = slice(c * LANES, (c + 1) * LANES)
        b, part = divmod(c, BS // LANES)
        lanes = slice(part * LANES, (part + 1) * LANES)
        blocks[b, :MODES, lanes] = residual_of(left, span).astype(BF16)
        blocks[NBR + 2 + b, :MODES, lanes] = residual_of(right, span).astype(BF16)
    for c in range(TILES):
        span = slice(c * LANES, (c + 1) * LANES)
        b, part = divmod(c, BS // LANES)
        lanes = slice(part * LANES, (part + 1) * LANES)
        value = residual_of(ratios, span)
        residual[:, span] = value
        blocks[b + 2, :MODES, lanes] = value.astype(BF16)
        other_t[span, :MODES] = residual_of(other, span).T
    copy = pltpu.make_async_copy(residual, residual_out, sem)
    copy.start()
    coup[...] = jnp.zeros_like(coup)
    gram[...] = jnp.zeros_like(gram)

    def blocked(index, carry):
        slots = UNROLL * SLOTS
        beside = coupler(index * slots, slots, 8, rows, rows_o, weights, other_t, coup)
        for u in range(UNROLL):
            b = index * UNROLL + u
            total = block_sum(b, b + 2, blocks, tables, flipped, kinds, scales, beside)
            image_r[:, pl.ds(pl.multiple_of(b * BS, BS), BS)] = total[:MODES]
        return carry

    lax.fori_loop(0, NBR // UNROLL, blocked, 0)
    for c in range(TILES):
        span = slice(c * LANES, (c + 1) * LANES)
        image_r[:, span] = image_r[:, span] + coup[span, :].T[:MODES]

    def step(b, carry):
        span = pl.ds(pl.multiple_of(b * 2 * BS, 2 * BS), 2 * BS)
        both = jnp.concatenate(
            [ref[:, span] for ref in (modes, residual, prev, image_x, image_r, image_p)], axis=0
        )
        high = both.astype(BF16)
        low = (both - high.astype(F32)).astype(BF16)
        gram[...] += lax.dot_general(
            jnp.concatenate([high, low], axis=0), high, (((1,), (1,)), ((), ())),
            preferred_element_type=F32,
        )
        return carry

    lax.fori_loop(0, NBR // 2, step, 0)
    n = 3 * MODES
    pad = LANES - n
    zero_r = jnp.zeros((pad, n), F32)
    zero_c = jnp.zeros((LANES, pad), F32)

    def square(top, lane):
        value = gram[top : top + n, lane : lane + n]
        return jnp.concatenate([jnp.concatenate([value, zero_r], axis=0), zero_c], axis=1)

    cross_b = square(2 * n, 0)
    gram_b = square(0, 0) + cross_b + cross_b.T
    cross_a = square(0, n) + square(2 * n, n)
    raw = cross_a + square(3 * n, 0).T
    gram_a = raw + raw.T
    row = lax.broadcasted_iota(jnp.int32, (LANES, LANES), 0)
    col = lax.broadcasted_iota(jnp.int32, (LANES, LANES), 1)
    diagonal = jnp.sum(jnp.where(row == col, gram_a, 0.0), axis=0, keepdims=True)
    merged = jnp.where(row >= col, gram_b, gram_a)
    packed[...] = jnp.where(row == n, jnp.broadcast_to(diagonal, (LANES, LANES)), merged)
    copy.wait()


def lower_inverse(gram, count):
    group = 4
    tiles = count // 8
    sub = lax.broadcasted_iota(jnp.int32, (8, LANES), 0)
    lane = lax.broadcasted_iota(jnp.int32, (8, LANES), 1)
    left = [gram[8 * t : 8 * t + 8, :] for t in range(tiles)]
    right = [jnp.where(lane == sub + 8 * t, 1.0, 0.0).astype(F32) for t in range(tiles)]

    def spread(first):
        return [
            {
                t: jnp.broadcast_to(left[t][:, first + m : first + m + 1], (8, LANES))
                for t in range(first // 8, tiles)
            }
            for m in range(group)
        ]

    ahead = spread(0)
    for start in range(0, count, group):
        now = ahead
        ahead = spread(start + group) if start + group < count else []
        for k in range(group):
            pivot = start + k
            tile, r = divmod(pivot, 8)
            root = lax.rsqrt(now[k][tile][r : r + 1, :])
            factor = {t: now[k][t] * root for t in range(tile, tiles)}
            factor[tile] = jnp.where(sub > r, factor[tile], 0.0)
            for first, columns in ((start, now), (start + group, ahead)):
                for m, column in enumerate(columns):
                    at = first + m
                    if at <= pivot:
                        continue
                    own = factor[at // 8][at % 8 : at % 8 + 1, :]
                    for t in column:
                        column[t] = column[t] - factor[t] * own
            line_l = left[tile][r : r + 1, :] * root
            line_r = right[tile][r : r + 1, :] * root
            for t in range(tile, tiles):
                left[t] = left[t] - factor[t] * line_l
                right[t] = right[t] - factor[t] * line_r
            right[tile] = jnp.where(sub == r, line_r, right[tile])
    return right


def final_kernel(packed, modes, residual_in, prev, basis, projected, result, residual, sems):
    n = 3 * MODES
    load = pltpu.make_async_copy(residual_in, residual, sems.at[ROWS // WIDTH])
    load.start()
    row = lax.broadcasted_iota(jnp.int32, (LANES, LANES), 0)
    col = lax.broadcasted_iota(jnp.int32, (LANES, LANES), 1)
    merged = packed[...]
    flipped = merged.T
    inside = (row < n) & (col < n)
    ndof = jnp.float32(2.0 * 64 * ROWS)
    gram_b = jnp.where(inside, jnp.where(row >= col, merged, flipped) / ndof, 0.0)
    diagonal = jnp.broadcast_to(merged[n : n + 1, :], (LANES, LANES))
    gram_a = jnp.where(row < col, merged, flipped)
    gram_a = jnp.where(row == col, diagonal, gram_a) / (2.0 * ndof)
    gram_a = jnp.where(inside, gram_a, 0.0)
    factors = jnp.concatenate(lower_inverse(gram_b, n), axis=0)
    half = lax.dot_general(
        factors, gram_a, (((1,), (0,)), ((), ())),
        precision=lax.Precision.HIGHEST, preferred_element_type=F32,
    )
    whole = lax.dot_general(
        half, factors, (((1,), (1,)), ((), ())),
        precision=lax.Precision.HIGHEST, preferred_element_type=F32,
    )
    projected[...] = whole
    factors = factors[:, :n]
    high = factors.astype(BF16)
    low = (factors - high.astype(F32)).astype(BF16)
    top = jnp.concatenate([high, high], axis=1)
    dims = (((1,), (0,)), ((), ()))
    load.wait()
    stores = []
    for index in range(ROWS // WIDTH):
        span = pl.ds(index * WIDTH, WIDTH)
        part = jnp.concatenate([modes[:, span], residual[:, span], prev[:, span]], axis=0)
        part_h = part.astype(BF16)
        part_l = (part - part_h.astype(F32)).astype(BF16)
        stacked = jnp.concatenate([part_h, part_l], axis=0)
        result[:, span] = lax.dot_general(
            top, stacked, dims, preferred_element_type=F32
        ) + lax.dot_general(low, part_h, dims, preferred_element_type=F32)
        store = pltpu.make_async_copy(
            result.at[:, span], basis.at[:, span], sems.at[index]
        )
        store.start()
        stores.append(store)
    for store in stores:
        store.wait()


def shards(modes, previous, kinds, scales, tables, wet_rows, wet_counts, coupling):
    modes = modes[0]
    prev = previous[0]
    kinds = kinds[0].reshape(3 * NBLK)
    scales = scales[0].reshape(3 * NBLK)
    tables = tables[0].reshape(3 * NTYPE, BS, BS)
    rows = wet_rows[0]
    modes, prev, whole, head, tail, weights, rows = rounded_parts(
        modes, prev, coupling, rows, wet_counts
    )
    weights = weights.reshape(IFACE)
    rows_o = swap_field(rows).reshape(IFACE)
    rows = rows.reshape(IFACE)
    other = swap_field(whole)
    left = from_left(tail)
    right = from_right(head)
    coupling_args = (rows, rows_o, weights)
    plane = shape(MODES, ROWS)
    rows_by_lanes = shape(ROWS, LANES)
    end = shape(PAIR, HALO)
    partial_x, partial_p, coup, tables, flipped = pl.pallas_call(
        inner_kernel,
        out_shape=(
            plane, plane, rows_by_lanes,
            shape(3 * NTYPE, BS, BS, kind=BF16), shape(2 * NTYPE, BS, BS, kind=BF16),
        ),
        in_specs=[VMEM] * 3 + [HBM] + [SMEM] * 5,
        out_specs=[VMEM] * 5,
        scratch_shapes=[
            pltpu.VMEM((NBR, PAIR, BS), BF16),
            pltpu.VMEM((ROWS, LANES), F32),
            pltpu.SemaphoreType.DMA(()),
        ],
        compiler_params=params(10),
        name="inner",
    )(modes, prev, other, in_hbm(tables), kinds, scales, *coupling_args)
    image_x, image_p, ratios, head, tail, sums = pl.pallas_call(
        outer_kernel,
        out_shape=(plane, plane, shape(PAIR, ROWS), end, end, shape(ALL_DEV, LANES)),
        in_specs=[VMEM] * 9 + [SMEM] * 2,
        out_specs=[VMEM] * 6,
        scratch_shapes=[pltpu.VMEM((12, PAIR, BS), BF16)],
        compiler_params=params(6),
        name="outer",
    )(modes, prev, left, right, partial_x, partial_p, coup, tables, flipped, kinds, scales)
    gathered = exchange(sums)
    residual, packed = pl.pallas_call(
        second_kernel,
        out_shape=(pltpu.HBM((MODES, ROWS), F32), shape(LANES, LANES)),
        in_specs=[VMEM] * 6 + [SMEM] * 5 + [VMEM] * 5,
        out_specs=[HBM, VMEM],
        scratch_shapes=[
            pltpu.VMEM((NBR + 4, SINGLE, BS), BF16),
            pltpu.VMEM((ROWS, LANES), F32),
            pltpu.VMEM((ROWS, LANES), F32),
            pltpu.VMEM((MODES, ROWS), F32),
            pltpu.VMEM((12 * MODES, 6 * MODES), F32),
            pltpu.VMEM((MODES, ROWS), F32),
            pltpu.SemaphoreType.DMA(()),
        ],
        compiler_params=params(18),
        name="second",
    )(
        gathered, ratios, from_left(tail), from_right(head), swap_field(ratios),
        tables, kinds, scales, *coupling_args,
        flipped, modes, prev, image_x, image_p,
    )
    part = jnp.sum(exchange(packed), axis=0, keepdims=True)
    packed = exchange(jnp.broadcast_to(part, (ALL_DEV, LANES)))
    n = 3 * MODES
    basis, projected = pl.pallas_call(
        final_kernel,
        out_shape=(pltpu.HBM((n, ROWS), F32), shape(n, n)),
        in_specs=[VMEM, VMEM, HBM, VMEM],
        out_specs=[HBM, VMEM],
        scratch_shapes=[
            pltpu.VMEM((n, ROWS), F32),
            pltpu.VMEM((MODES, ROWS), F32),
            pltpu.SemaphoreType.DMA((ROWS // WIDTH + 1,)),
        ],
        compiler_params=params(14),
        name="final",
    )(packed, modes, in_hbm(residual), prev)
    return (basis[None], projected)


def solution(mesh):
    finer = Mesh(
        mesh.devices.reshape(mesh.shape["field"], 4, 4, 4), ("field", "dom_0", "dom_1", "dom_2")
    )
    placed = (
        P("field", None, DOM),
        P("field", None, DOM),
        P("field", None, None),
        P("field", None, None),
        P("field", None, None, None, None),
        P("field", DOM),
        P(DOM),
        P(DOM),
    )
    return jax.shard_map(
        shards, mesh=finer, in_specs=placed, out_specs=(P("field", None, DOM), P()), check_vma=False
    )
```

profile of v0, /device:TPU:1, one launch (start us, length us, event | category | flops | bytes accessed | tf_op | source)
XLA Modules:
  0.0 109.9 jit_solution(11488098526300651668)
XLA Ops:
  1.3 0.0 copy-start
  1.3 0.0 copy-start.1
  1.3 1.9 %rounded.1 = (f32[40,8192]{1,0:T(8,128)S(1)}, f32[40,8192]{1,0:T(8,128)S(1)}, bf16[80,8192]{1,0:T(8,128)(2,1)S(1)}, bf16[80,1024]{1,0:T(8,128)(2,1)S(1)}, bf16[8...) custom-call(f32[40,8192]{1,0:T(8,128)} %bitcast.36, f32[40,8192]{1,0:T(8,128)} %bitcast.37, ...), custom_call_target="tpu_custom_call" | custom-call | tf_op jit(solution)/shard_map/rounded/pallas_call | solution.py:97
  3.2 1.5 %collective-permute-start.2 = (bf16[80,8192]{1,0:T(8,128)(2,1)S(1)}, bf16[80,8192]{1,0:T(8,128)(2,1)S(1)}, u32[]{:S(2)}, u32[]{:S(2)}) collective-permute-start(bf16[80,8192]{1,0:T(8,128)(2,1)S(1)} %get-tuple-element.28), channel_id=1, source_target_pairs={{0,64},{64,0},{1,65},{65,1},{2,66},{66,2},{3,67},{67,3},{4,68},{68... | collective-permute-start | bytes 3932168 | tf_op jit(solution)/shard_map/ppermute | solution.py:55
  4.7 3.7 %collective-permute-start = (bf16[80,1024]{1,0:T(8,128)(2,1)S(1)}, bf16[80,1024]{1,0:T(8,128)(2,1)S(1)}, u32[]{:S(2)}, u32[]{:S(2)}) collective-permute-start(bf16[80,1024]{1,0:T(8,128)(2,1)S(1)} %get-tuple-element.26), channel_id=1, source_target_pairs={{0,1},{1,2},{2,3},{3,4},{4,5},{5,6},{6,7},{7,8},{8,9},{9,10},{10,1... | collective-permute-start | bytes 491528 | tf_op jit(solution)/shard_map/ppermute | solution.py:59
  8.3 1.3 %collective-permute-start.1 = (bf16[80,1024]{1,0:T(8,128)(2,1)S(1)}, bf16[80,1024]{1,0:T(8,128)(2,1)S(1)}, u32[]{:S(2)}, u32[]{:S(2)}) collective-permute-start(bf16[80,1024]{1,0:T(8,128)(2,1)S(1)} %get-tuple-element.27), channel_id=1, source_target_pairs={{1,0},{2,1},{3,2},{4,3},{5,4},{6,5},{7,6},{8,7},{9,8},{10,9},{11,1... | collective-permute-start | bytes 491528 | tf_op jit(solution)/shard_map/ppermute | solution.py:63
  9.6 0.4 collective-permute-start.3
  10.0 0.9 collective-permute-done.3
  10.9 0.0 collective-permute-done.2.other
  10.9 0.0 copy-done
  10.9 0.0 copy-done.1
  10.9 13.5 %inner.1 = (f32[40,8192]{1,0:T(8,128)S(1)}, f32[40,8192]{1,0:T(8,128)S(1)}, f32[8192,128]{1,0:T(8,128)S(1)}, bf16[12,512,512]{2,1,0:T(8,128)(2,1)S(1)}, bf16[8,512,512]{2,1,0:T(8,128)(2,1)S(1)}) custom-call(f32[40,8192]{1,0:T(8,128)S(1)} %get-tuple-element.24.modes, f32[40,8192]{1,0:T(8,128)S(1)} %get-tuple-element.25.prev, ...), custom_call_target="tpu_custom_call" | custom-call | tf_op jit(solution)/shard_map/inner/pallas_call | solution.py:441
  24.4 0.0 collective-permute-done.left
  24.5 0.0 collective-permute-done.1.right
  24.5 4.5 %outer.1 = (f32[40,8192]{1,0:T(8,128)S(1)}, f32[40,8192]{1,0:T(8,128)S(1)}, f32[80,8192]{1,0:T(8,128)S(1)}, f32[80,1024]{1,0:T(8,128)S(1)}, f32[80,1024]{1,0:T(8,128)S(1)}, /*index=5*/f32[128,128]{1,0:T(8,128)S(1)}) custom-call(f32[40,8192]{1,0:T(8,128)S(1)} %get-tuple-element.24.modes, f32[40,8192]{1,0:T(8,128)S(1)} %get-tuple-element.25.prev, ...), custom_call_target="tpu_custom_call" | custom-call | tf_op jit(solution)/shard_map/outer/pallas_call | solution.py:457
  28.9 0.4 collective-permute-start.6
  29.3 4.3 %collective-permute-start.4 = (f32[80,1024]{1,0:T(8,128)S(1)}, f32[80,1024]{1,0:T(8,128)S(1)}, u32[]{:S(2)}, u32[]{:S(2)}) collective-permute-start(f32[80,1024]{1,0:T(8,128)S(1)} %get-tuple-element.38), channel_id=1, source_target_pairs={{0,1},{1,2},{2,3},{3,4},{4,5},{5,6},{6,7},{7,8},{8,9},{9,10},{10,1... | collective-permute-start | bytes 983048 | tf_op jit(solution)/shard_map/ppermute | solution.py:59
  33.6 1.3 %collective-permute-start.5 = (f32[80,1024]{1,0:T(8,128)S(1)}, f32[80,1024]{1,0:T(8,128)S(1)}, u32[]{:S(2)}, u32[]{:S(2)}) collective-permute-start(f32[80,1024]{1,0:T(8,128)S(1)} %get-tuple-element.39), channel_id=1, source_target_pairs={{1,0},{2,1},{3,2},{4,3},{5,4},{6,5},{7,6},{8,7},{9,8},{10,9},{11,1... | collective-permute-start | bytes 983048 | tf_op jit(solution)/shard_map/ppermute | solution.py:63
  34.9 22.9 %all_to_all.28 = f32[128,1,128]{2,1,0:T(1,128)S(1)} all-to-all(f32[128,1,128]{2,1,0:T(1,128)S(1)} %bitcast.27), channel_id=1, replica_groups=mesh['field'=2,'dom_0'=4,'dom_1'=4,'dom_2'=4] {'field','dom_0','dom_1','..., dimensions={0} | all-to-all | bytes 131072 | tf_op jit(solution)/shard_map/all_to_all | solution.py:67
  57.9 0.0 collective-permute-done.4.left
  57.9 0.0 collective-permute-done.5.right
  57.9 0.0 collective-permute-done.6.other
  57.9 16.5 %second.1 = (f32[40,8192]{1,0:T(8,128)}, f32[128,128]{1,0:T(8,128)S(1)}) custom-call(f32[128,128]{1,0:T(8,128)S(1)} %bitcast.19, f32[80,8192]{1,0:T(8,128)S(1)} %get-tuple-element.37.ratios, f32[80,1024]{1,0:T(8,128)S(1)} %collective-permute-done.4.left, f32[80,1024]{1,0:T(8,128)S(1)} %collective-permute-done.5.right, ...), custom_call_target="tpu_custom_call" | custom-call | tf_op jit(solution)/shard_map/second/pallas_call | solution.py:467
  74.3 14.9 %all_to_all.29 = f32[128,1,128]{2,1,0:T(1,128)S(1)} all-to-all(f32[128,1,128]{2,1,0:T(1,128)S(1)} %bitcast.28), channel_id=1, replica_groups=mesh['field'=2,'dom_0'=4,'dom_1'=4,'dom_2'=4] {'field','dom_0','dom_1','..., dimensions={0} | all-to-all | bytes 131072 | tf_op jit(solution)/shard_map/all_to_all | solution.py:67
  89.2 0.2 reduce_sum.9
  89.4 13.8 %all_to_all.30 = f32[128,1,128]{2,1,0:T(1,128)S(1)} all-to-all(f32[128,1,128]{2,1,0:T(1,128)S(1)} %broadcast_in_dim.4), channel_id=1, replica_groups=mesh['field'=2,'dom_0'=4,'dom_1'=4,'dom_2'=4] {'field','dom_0','dom_1','..., dimensions={0} | all-to-all | bytes 131072 | tf_op jit(solution)/shard_map/all_to_all | solution.py:67
  103.2 6.5 %final.1 = (f32[120,8192]{1,0:T(8,128)}, f32[120,120]{1,0:T(8,128)}) custom-call(f32[128,128]{1,0:T(8,128)S(1)} %bitcast.20, f32[40,8192]{1,0:T(8,128)S(1)} %get-tuple-element.24.modes, f32[40,8192]{1,0:T(8,128)} %get-tuple-element.43.residual_in, f32[40,8192]{1,0:T(8,128)S(1)} %get-tuple-element.25.prev), custom_call_target="tpu_custom_call" | custom-call | tf_op jit(solution)/shard_map/final/pallas_call | solution.py:491
  (1 shorter events, 0.0 us)
Async XLA Ops:
  1.3 9.6 %copy-start = (s32[1,3,1024]{2,0,1:T(1,128)S(1)}, s32[1,3,1024]{2,0,1:T(1,128)}, u32[]{:S(2)}) copy-start(s32[1,3,1024]{2,0,1:T(1,128)} %param.10) | copy-start | bytes 36868
  1.3 9.6 %copy-start.1 = (f32[1,3,1024]{2,0,1:T(1,128)S(1)}, f32[1,3,1024]{2,0,1:T(1,128)}, u32[]{:S(2)}) copy-start(f32[1,3,1024]{2,0,1:T(1,128)} %param.11) | copy-start | bytes 36868
  3.2 7.7 %collective-permute-start.2 = (bf16[80,8192]{1,0:T(8,128)(2,1)S(1)}, bf16[80,8192]{1,0:T(8,128)(2,1)S(1)}, u32[]{:S(2)}, u32[]{:S(2)}) collective-permute-start(bf16[80,8192]{1,0:T(8,128)(2,1)S(1)} %get-tuple-element.28), channel_id=1, source_target_pairs={{0,64},{64,0},{1,65},{65,1},{2,66},{66,2},{3,67},{67,3},{4,68},{68... | collective-permute-start | bytes 3932168 | tf_op jit(solution)/shard_map/ppermute | solution.py:55
  4.7 19.8 %collective-permute-start = (bf16[80,1024]{1,0:T(8,128)(2,1)S(1)}, bf16[80,1024]{1,0:T(8,128)(2,1)S(1)}, u32[]{:S(2)}, u32[]{:S(2)}) collective-permute-start(bf16[80,1024]{1,0:T(8,128)(2,1)S(1)} %get-tuple-element.26), channel_id=1, source_target_pairs={{0,1},{1,2},{2,3},{3,4},{4,5},{5,6},{6,7},{7,8},{8,9},{9,10},{10,1... | collective-permute-start | bytes 491528 | tf_op jit(solution)/shard_map/ppermute | solution.py:59
  8.3 16.1 %collective-permute-start.1 = (bf16[80,1024]{1,0:T(8,128)(2,1)S(1)}, bf16[80,1024]{1,0:T(8,128)(2,1)S(1)}, u32[]{:S(2)}, u32[]{:S(2)}) collective-permute-start(bf16[80,1024]{1,0:T(8,128)(2,1)S(1)} %get-tuple-element.27), channel_id=1, source_target_pairs={{1,0},{2,1},{3,2},{4,3},{5,4},{6,5},{7,6},{8,7},{9,8},{10,9},{11,1... | collective-permute-start | bytes 491528 | tf_op jit(solution)/shard_map/ppermute | solution.py:63
  9.6 1.3 %collective-permute-start.3 = (s32[24,128]{1,0:T(8,128)S(1)}, s32[24,128]{1,0:T(8,128)S(1)}, u32[]{:S(2)}, u32[]{:S(2)}) collective-permute-start(s32[24,128]{1,0:T(8,128)S(1)} %get-tuple-element.29), channel_id=1, source_target_pairs={{0,64},{64,0},{1,65},{65,1},{2,66},{66,2},{3,67},{67,3},{4,68},{68... | collective-permute-start | bytes 36872 | tf_op jit(solution)/shard_map/ppermute | solution.py:55
  28.9 28.9 %collective-permute-start.6 = (f32[80,8192]{1,0:T(8,128)S(1)}, f32[80,8192]{1,0:T(8,128)S(1)}, u32[]{:S(2)}, u32[]{:S(2)}) collective-permute-start(f32[80,8192]{1,0:T(8,128)S(1)} %get-tuple-element.37.ratios), channel_id=1, source_target_pairs={{0,64},{64,0},{1,65},{65,1},{2,66},{66,2},{3,67},{67,3},{4,68},{68... | collective-permute-start | bytes 7864328 | tf_op jit(solution)/shard_map/ppermute | solution.py:55
  29.3 28.5 %collective-permute-start.4 = (f32[80,1024]{1,0:T(8,128)S(1)}, f32[80,1024]{1,0:T(8,128)S(1)}, u32[]{:S(2)}, u32[]{:S(2)}) collective-permute-start(f32[80,1024]{1,0:T(8,128)S(1)} %get-tuple-element.38), channel_id=1, source_target_pairs={{0,1},{1,2},{2,3},{3,4},{4,5},{5,6},{6,7},{7,8},{8,9},{9,10},{10,1... | collective-permute-start | bytes 983048 | tf_op jit(solution)/shard_map/ppermute | solution.py:59
  33.6 24.2 %collective-permute-start.5 = (f32[80,1024]{1,0:T(8,128)S(1)}, f32[80,1024]{1,0:T(8,128)S(1)}, u32[]{:S(2)}, u32[]{:S(2)}) collective-permute-start(f32[80,1024]{1,0:T(8,128)S(1)} %get-tuple-element.39), channel_id=1, source_target_pairs={{1,0},{2,1},{3,2},{4,3},{5,4},{6,5},{7,6},{8,7},{9,8},{10,9},{11,1... | collective-permute-start | bytes 983048 | tf_op jit(solution)/shard_map/ppermute | solution.py:63
where the time goes:
time: 110 us
  blocking collectives  51.6 us (47%)
  Pallas kernels  42.9 us (39%)
  starting transfers between devices  12.8 us (12%)
  between operations  1.55 us (1%)
    all_to_all x3, blocking collectives, exchange(): return lax.all_to_all(rows, FIELD_DOM, 0, 0, tiled=True)  51.6 us
    pallas_call x1, Pallas kernels, shards(): pl.pallas_call(second_kernel, out_shape=(pltpu.HBM((MODES, ROWS), F32), s...  16.5 us
    pallas_call x1, Pallas kernels, shards(): pl.pallas_call(inner_kernel, out_shape=(plane, plane, rows_by_lanes, shap...  13.5 us
    ppermute x2, starting transfers between devices, from_left(): return lax.ppermute(value, DOM, [(i, i + 1) for i in range(63)])  7.94 us
    pallas_call x1, Pallas kernels, shards(): pl.pallas_call(final_kernel, out_shape=(pltpu.HBM((n, ROWS), F32), shape(...  6.49 us
    pallas_call x1, Pallas kernels, shards(): pl.pallas_call(outer_kernel, out_shape=(plane, plane, shape(PAIR, ROWS),...  4.47 us
    ppermute x2, starting transfers between devices, from_right(): return lax.ppermute(value, DOM, [(i + 1, i) for i in range(63)])  2.58 us
    ppermute x3, starting transfers between devices, swap_field(): return lax.ppermute(value, 'field', [(0, 1), (1, 0)])  2.23 us
  transfers between devices with their start and end apart: 7, of which 1 were waited for; matrix products, arithmetic and copies ran while one was open for 0% of the time, Pallas kernels for 12%

commit v1 on v0

--- a/solution.py
+++ b/solution.py
@@ -28,8 +28,8 @@
 HBM = pl.BlockSpec(memory_space=pltpu.HBM)
 PAIR = 2 * MODES
 SINGLE = 48
-UNROLL = 2
-SLOTS = IFACE // NBR
+INNER = 6
+ENDS = ((2, 0), (3, 1), (4, 2), (5, 3), (6, 12), (7, 13), (8, 14), (9, 15))
 WIDTH = 1024
 
 OPS = ((0, 0, 0, 0), (1, -1, -1, 0), (2, -2, -2, 0), (1, 1, 0, 1), (2, 2, 0, 1))
@@ -128,14 +128,15 @@
 
 
 def coupler(base, total, dots, rows, rows_o, weights, other_t, coup):
-    share = total // dots
+    cuts = [total * index // dots for index in range(dots + 1)]
     taken = []
 
     def beside(_, value):
         if len(taken) == dots:
             return
         late = jnp.where(value == value, 0, 1)
-        start = jnp.minimum(base + len(taken) * share + late, IFACE - share)
+        cut, share = cuts[len(taken)], cuts[len(taken) + 1] - cuts[len(taken)]
+        start = jnp.minimum(base + cut + late, IFACE - share)
         taken.append(start)
         for v in range(share):
             slot = start + v
@@ -146,10 +147,18 @@
 
 def inner_kernel(
     modes, prev, other, tables_in, kinds, scales, rows, rows_o, weights,
-    partial_x, partial_p, coup, tables, flipped, blocks, other_t, sem,
+    partial_x, partial_p, coup, tables, flipped, blocks, other_t, sems,
 ):
-    load = pltpu.make_async_copy(tables_in, tables, sem)
-    load.start()
+    loads = [
+        pltpu.make_async_copy(
+            tables_in.at[pl.ds(offset * NTYPE, NTYPE)],
+            tables.at[pl.ds(offset * NTYPE, NTYPE)],
+            sems.at[offset],
+        )
+        for offset in range(3)
+    ]
+    for offset in (1, 2, 0):
+        loads[offset].start()
     for b in range(NBR):
         span = slice(b * BS, (b + 1) * BS)
         blocks[b] = jnp.concatenate([modes[:, span], prev[:, span]], axis=0).astype(BF16)
@@ -157,16 +166,18 @@
         span = slice(c * LANES, (c + 1) * LANES)
         other_t[span, :PAIR] = other[:, span].astype(F32).T
     coup[...] = jnp.zeros_like(coup)
-    load.wait()
-    for index in range(2 * NTYPE):
-        flipped[index] = tables[NTYPE + index].T
-    steps = (NBR - 4) // UNROLL
+    for offset in (1, 2):
+        loads[offset].wait()
+        for index in range(NTYPE):
+            flipped[(offset - 1) * NTYPE + index] = tables[offset * NTYPE + index].T
+    loads[0].wait()
+    steps = (NBR - 4) // INNER
     slots = IFACE // steps
 
     def step(index, carry):
-        beside = coupler(index * slots, slots, 8, rows, rows_o, weights, other_t, coup)
-        for u in range(UNROLL):
-            b = 2 + index * UNROLL + u
+        beside = coupler(index * slots, slots, 5 * INNER - 1, rows, rows_o, weights, other_t, coup)
+        for u in range(INNER):
+            b = 2 + index * INNER + u
             total = block_sum(b, b, blocks, tables, flipped, kinds, scales, beside)
             span = pl.ds(pl.multiple_of(b * BS, BS), BS)
             partial_x[:, span] = total[:MODES]
@@ -178,14 +189,14 @@
 
 def outer_kernel(
     modes, prev, left, right, partial_x, partial_p, coup, tables, flipped, kinds, scales,
-    image_x, image_p, ratios, head, tail, sums, ends,
+    image_x, image_p, inverse_j, sums, ends,
 ):
     first = domain_index() * NBR
     for b in range(2):
         span = slice(b * BS, (b + 1) * BS)
         ends[b] = left[:, span]
         ends[10 + b] = right[:, span]
-    for at, b in ((2, 0), (3, 1), (4, 2), (5, 3), (6, 12), (7, 13), (8, 14), (9, 15)):
+    for at, b in ENDS:
         span = slice(b * BS, (b + 1) * BS)
         ends[at] = jnp.concatenate([modes[:, span], prev[:, span]], axis=0).astype(BF16)
 
@@ -194,8 +205,8 @@
             b = index * (NBR - 2) + u
             total = block_sum(b, 2 + index * 6 + u, ends, tables, flipped, kinds, scales)
             span = pl.ds(pl.multiple_of(b * BS, BS), BS)
-            partial_x[:, span] = total[:MODES]
-            partial_p[:, span] = total[MODES:]
+            image_x[:, span] = total[:MODES]
+            image_p[:, span] = total[MODES:]
         return carry
 
     lax.fori_loop(0, 2, step, 0)
@@ -220,9 +231,10 @@
         b, part = divmod(c, BS // LANES)
         span = slice(c * LANES, (c + 1) * LANES)
         coupled = coup[span, :].T
-        value = partial_x[:, span] + coupled[:MODES]
+        source_x, source_p = (partial_x, partial_p) if 2 <= b < NBR - 2 else (image_x, image_p)
+        value = source_x[:, span] + coupled[:MODES]
         image_x[:, span] = value
-        image_p[:, span] = partial_p[:, span] + coupled[MODES:PAIR]
+        image_p[:, span] = source_p[:, span] + coupled[MODES:PAIR]
         own = modes[:, span]
         squares += own * own
         crossed += own * value
@@ -230,78 +242,101 @@
         line = lines[part][0]
         for other_kind in range(1, NTYPE):
             line = jnp.where(kind == other_kind, lines[part][other_kind], line)
-        inverse = 1.0 / (scales[first + b] * line)
-        ratio = jnp.concatenate([value * inverse, own * inverse], axis=0)
-        ratios[:, span] = ratio
-        if c < HALO // LANES:
-            head[:, span] = ratio
-        if c >= TILES - HALO // LANES:
-            at = (c - (TILES - HALO // LANES)) * LANES
-            tail[:, at : at + LANES] = ratio
+        inverse_j[:, span] = 1.0 / (scales[first + b] * line)
     both = jnp.concatenate([squares, crossed, jnp.zeros((LANES - PAIR, LANES), F32)], axis=0)
     total = jnp.sum(both.T, axis=0, keepdims=True)
     sums[...] = jnp.broadcast_to(total, (ALL_DEV, LANES))
 
 
-def second_kernel(
-    gathered, ratios, left, right, other, tables, kinds, scales, rows, rows_o, weights,
-    flipped, modes, prev, image_x, image_p, residual_out, packed,
-    blocks, other_t, coup, image_r, gram, residual, sem,
-):
+def residual_kernel(gathered, modes, image_x, inverse_j, residual, whole, head, tail):
     total = jnp.sum(gathered[...], axis=0, keepdims=True)
     column = jnp.broadcast_to(total, (LANES, LANES)).T
     quotient = column[MODES:PAIR, :] / column[:MODES, :]
-
-    def residual_of(source, span):
-        return source[:MODES, span] - source[MODES:, span] * quotient
-
-    for c in range(HALO // LANES):
-        span = slice(c * LANES, (c + 1) * LANES)
-        b, part = divmod(c, BS // LANES)
-        lanes = slice(part * LANES, (part + 1) * LANES)
-        blocks[b, :MODES, lanes] = residual_of(left, span).astype(BF16)
-        blocks[NBR + 2 + b, :MODES, lanes] = residual_of(right, span).astype(BF16)
     for c in range(TILES):
         span = slice(c * LANES, (c + 1) * LANES)
-        b, part = divmod(c, BS // LANES)
-        lanes = slice(part * LANES, (part + 1) * LANES)
-        value = residual_of(ratios, span)
+        value = (image_x[:, span] - modes[:, span] * quotient) * inverse_j[:, span]
         residual[:, span] = value
-        blocks[b + 2, :MODES, lanes] = value.astype(BF16)
-        other_t[span, :MODES] = residual_of(other, span).T
+        low = value.astype(BF16)
+        whole[:, span] = low
+        if c < HALO // LANES:
+            head[:, span] = low
+        if c >= TILES - HALO // LANES:
+            at = (c - (TILES - HALO // LANES)) * LANES
+            tail[:, at : at + LANES] = low
+
+
+def inner_second_kernel(
+    whole, other, tables, flipped, kinds, scales, rows, rows_o, weights,
+    partial, coup, blocks, other_t,
+):
+    for b in range(NBR):
+        blocks[b, :MODES] = whole[:, b * BS : (b + 1) * BS]
+    for c in range(TILES):
+        span = slice(c * LANES, (c + 1) * LANES)
+        other_t[span, :MODES] = other[:, span].astype(F32).T
+    coup[...] = jnp.zeros_like(coup)
+    steps = (NBR - 4) // INNER
+    slots = IFACE // steps
+
+    def blocked(index, carry):
+        beside = coupler(index * slots, slots, 5 * INNER - 1, rows, rows_o, weights, other_t, coup)
+        for u in range(INNER):
+            b = 2 + index * INNER + u
+            total = block_sum(b, b, blocks, tables, flipped, kinds, scales, beside)
+            partial[:, pl.ds(pl.multiple_of(b * BS, BS), BS)] = total[:MODES]
+        return carry
+
+    lax.fori_loop(0, steps, blocked, 0)
+
+
+def outer_second_kernel(
+    residual, whole, left, right, partial, coup, tables, flipped, kinds, scales,
+    modes, prev, image_x, image_p, residual_out, packed, ends, image_e, gram, sem,
+):
     copy = pltpu.make_async_copy(residual, residual_out, sem)
     copy.start()
-    coup[...] = jnp.zeros_like(coup)
+    for b in range(2):
+        span = slice(b * BS, (b + 1) * BS)
+        ends[b, :MODES] = left[:, span]
+        ends[10 + b, :MODES] = right[:, span]
+    for at, b in ENDS:
+        ends[at, :MODES] = whole[:, b * BS : (b + 1) * BS]
     gram[...] = jnp.zeros_like(gram)
 
     def blocked(index, carry):
-        slots = UNROLL * SLOTS
-        beside = coupler(index * slots, slots, 8, rows, rows_o, weights, other_t, coup)
-        for u in range(UNROLL):
-            b = index * UNROLL + u
-            total = block_sum(b, b + 2, blocks, tables, flipped, kinds, scales, beside)
-            image_r[:, pl.ds(pl.multiple_of(b * BS, BS), BS)] = total[:MODES]
+        for u in range(2):
+            b = index * (NBR - 2) + u
+            total = block_sum(b, 2 + index * 6 + u, ends, tables, flipped, kinds, scales)
+            at = (index * 2 + u) * BS
+            image_e[:, pl.ds(pl.multiple_of(at, BS), BS)] = total[:MODES]
         return carry
 
-    lax.fori_loop(0, NBR // UNROLL, blocked, 0)
-    for c in range(TILES):
-        span = slice(c * LANES, (c + 1) * LANES)
-        image_r[:, span] = image_r[:, span] + coup[span, :].T[:MODES]
-
-    def step(b, carry):
+    lax.fori_loop(0, 2, blocked, 0)
+
+    def add(b, block_part):
         span = pl.ds(pl.multiple_of(b * 2 * BS, 2 * BS), 2 * BS)
-        both = jnp.concatenate(
-            [ref[:, span] for ref in (modes, residual, prev, image_x, image_r, image_p)], axis=0
-        )
+        coupled = [
+            coup[pl.ds(pl.multiple_of(b * 2 * BS + c * LANES, LANES), LANES), :].T[:MODES]
+            for c in range(2 * BS // LANES)
+        ]
+        image = block_part + jnp.concatenate(coupled, axis=1)
+        parts = [ref[:, span] for ref in (modes, residual, prev, image_x)]
+        both = jnp.concatenate([*parts, image, image_p[:, span]], axis=0)
         high = both.astype(BF16)
         low = (both - high.astype(F32)).astype(BF16)
         gram[...] += lax.dot_general(
             jnp.concatenate([high, low], axis=0), high, (((1,), (1,)), ((), ())),
             preferred_element_type=F32,
         )
+
+    def step(b, carry):
+        add(b, partial[:, pl.ds(pl.multiple_of(b * 2 * BS, 2 * BS), 2 * BS)])
         return carry
 
-    lax.fori_loop(0, NBR // 2, step, 0)
+    last = NBR // 2 - 1
+    add(0, image_e[:, : 2 * BS])
+    lax.fori_loop(1, last, step, 0)
+    add(last, image_e[:, 2 * BS :])
     n = 3 * MODES
     pad = LANES - n
     zero_r = jnp.zeros((pad, n), F32)
@@ -449,41 +484,61 @@
         scratch_shapes=[
             pltpu.VMEM((NBR, PAIR, BS), BF16),
             pltpu.VMEM((ROWS, LANES), F32),
-            pltpu.SemaphoreType.DMA(()),
+            pltpu.SemaphoreType.DMA((3,)),
         ],
         compiler_params=params(10),
         name="inner",
     )(modes, prev, other, in_hbm(tables), kinds, scales, *coupling_args)
-    image_x, image_p, ratios, head, tail, sums = pl.pallas_call(
+    image_x, image_p, inverse_j, sums = pl.pallas_call(
         outer_kernel,
-        out_shape=(plane, plane, shape(PAIR, ROWS), end, end, shape(ALL_DEV, LANES)),
+        out_shape=(plane, plane, shape(1, ROWS), shape(ALL_DEV, LANES)),
         in_specs=[VMEM] * 9 + [SMEM] * 2,
-        out_specs=[VMEM] * 6,
+        out_specs=[VMEM] * 4,
         scratch_shapes=[pltpu.VMEM((12, PAIR, BS), BF16)],
         compiler_params=params(6),
         name="outer",
     )(modes, prev, left, right, partial_x, partial_p, coup, tables, flipped, kinds, scales)
     gathered = exchange(sums)
+    end = shape(MODES, HALO, kind=BF16)
+    residual, whole, head, tail = pl.pallas_call(
+        residual_kernel,
+        out_shape=(plane, shape(MODES, ROWS, kind=BF16), end, end),
+        in_specs=[VMEM] * 4,
+        out_specs=[VMEM] * 4,
+        compiler_params=params(6),
+        name="residual",
+    )(gathered, modes, image_x, inverse_j)
+    other = swap_field(whole)
+    left = from_left(tail)
+    right = from_right(head)
+    partial, coup = pl.pallas_call(
+        inner_second_kernel,
+        out_shape=(plane, rows_by_lanes),
+        in_specs=[VMEM] * 4 + [SMEM] * 5,
+        out_specs=[VMEM] * 2,
+        scratch_shapes=[
+            pltpu.VMEM((NBR, SINGLE, BS), BF16),
+            pltpu.VMEM((ROWS, LANES), F32),
+        ],
+        compiler_params=params(10),
+        name="inner_second",
+    )(whole, other, tables, flipped, kinds, scales, *coupling_args)
     residual, packed = pl.pallas_call(
-        second_kernel,
+        outer_second_kernel,
         out_shape=(pltpu.HBM((MODES, ROWS), F32), shape(LANES, LANES)),
-        in_specs=[VMEM] * 6 + [SMEM] * 5 + [VMEM] * 5,
+        in_specs=[VMEM] * 8 + [SMEM] * 2 + [VMEM] * 4,
         out_specs=[HBM, VMEM],
         scratch_shapes=[
-            pltpu.VMEM((NBR + 4, SINGLE, BS), BF16),
-            pltpu.VMEM((ROWS, LANES), F32),
-            pltpu.VMEM((ROWS, LANES), F32),
-            pltpu.VMEM((MODES, ROWS), F32),
+            pltpu.VMEM((12, SINGLE, BS), BF16),
+            pltpu.VMEM((MODES, 4 * BS), F32),
             pltpu.VMEM((12 * MODES, 6 * MODES), F32),
-            pltpu.VMEM((MODES, ROWS), F32),
             pltpu.SemaphoreType.DMA(()),
         ],
-        compiler_params=params(18),
-        name="second",
+        compiler_params=params(10),
+        name="outer_second",
     )(
-        gathered, ratios, from_left(tail), from_right(head), swap_field(ratios),
-        tables, kinds, scales, *coupling_args,
-        flipped, modes, prev, image_x, image_p,
+        residual, whole, left, right, partial, coup, tables, flipped, kinds, scales,
+        modes, prev, image_x, image_p,
     )
     part = jnp.sum(exchange(packed), axis=0, keepdims=True)
     packed = exchange(jnp.broadcast_to(part, (ALL_DEV, LANES)))

time: 110 us -> 108 us (0.982)
  Pallas kernels: 42.9 us -> 41.3 us
  starting transfers between devices: 12.8 us -> 11.5 us
    pallas_call x1, Pallas kernels: 13.5 us -> 11.5 us  [shards(): pl.pallas_call(inner_kernel, out_shape=(plane, plane, rows_by_lanes, shap...]
    ppermute x2, starting transfers between devices: 7.94 us -> 6.1 us  [from_left(): return lax.ppermute(value, DOM, [(i, i + 1) for i in range(63)])]
    pallas_call x2 -> x4, Pallas kernels: 20.9 us -> 21.4 us  [the longest x1 8.9 us: shards(): pl.pallas_call(inner_second_kernel, out_shape=(plane, rows_by_lanes), in_...]
  transfers between devices with their start and end apart: 7 -> 7, of which waited for: 1 -> 1; matrix products, arithmetic and copies ran while one was open for 0% -> 0% of each run, Pallas kernels for 12% -> 19%
where the time goes in v1:
time: 108 us; the launch traced here: 107 us
  blocking collectives  51.8 us (48%)
  Pallas kernels  41.3 us (38%)
  starting transfers between devices  11.5 us (11%)
  between operations  1.58 us (1%)
    all_to_all x3, blocking collectives, exchange(): return lax.all_to_all(rows, FIELD_DOM, 0, 0, tiled=True)  51.8 us
    pallas_call x1, Pallas kernels, shards(): pl.pallas_call(inner_kernel, out_shape=(plane, plane, rows_by_lanes, shap...  11.5 us
    pallas_call x1, Pallas kernels, shards(): pl.pallas_call(inner_second_kernel, out_shape=(plane, rows_by_lanes), in_...  8.9 us
    pallas_call x1, Pallas kernels, shards(): pl.pallas_call(outer_second_kernel, out_shape=(pltpu.HBM((MODES, ROWS), F...  7.62 us
    pallas_call x1, Pallas kernels, shards(): pl.pallas_call(final_kernel, out_shape=(pltpu.HBM((n, ROWS), F32), shape(...  6.49 us
    ppermute x2, starting transfers between devices, from_left(): return lax.ppermute(value, DOM, [(i, i + 1) for i in range(63)])  6.1 us
    pallas_call x1, Pallas kernels, shards(): pl.pallas_call(outer_kernel, out_shape=(plane, plane, shape(1, ROWS), sha...  4.53 us
    ppermute x2, starting transfers between devices, from_right(): return lax.ppermute(value, DOM, [(i + 1, i) for i in range(63)])  2.76 us
  transfers between devices with their start and end apart: 7, of which 1 were waited for; matrix products, arithmetic and copies ran while one was open for 0% of the time, Pallas kernels for 19%

profile of v1, /device:TPU:1, one launch (start us, length us, event | category | flops | bytes accessed | tf_op | source)
XLA Modules:
  0.0 107.3 jit_solution(2026797790813231932)
XLA Ops:
  1.3 0.0 copy-start
  1.3 0.0 copy-start.1
  1.3 1.9 %rounded.1 = (f32[40,8192]{1,0:T(8,128)S(1)}, f32[40,8192]{1,0:T(8,128)S(1)}, bf16[80,8192]{1,0:T(8,128)(2,1)S(1)}, bf16[80,1024]{1,0:T(8,128)(2,1)S(1)}, bf16[8...) custom-call(f32[40,8192]{1,0:T(8,128)} %bitcast.38, f32[40,8192]{1,0:T(8,128)} %bitcast.39, ...), custom_call_target="tpu_custom_call" | custom-call | tf_op jit(solution)/shard_map/rounded/pallas_call | solution.py:97
  3.2 1.5 %collective-permute-start.2 = (bf16[80,8192]{1,0:T(8,128)(2,1)S(1)}, bf16[80,8192]{1,0:T(8,128)(2,1)S(1)}, u32[]{:S(2)}, u32[]{:S(2)}) collective-permute-start(bf16[80,8192]{1,0:T(8,128)(2,1)S(1)} %get-tuple-element.32), channel_id=1, source_target_pairs={{0,64},{64,0},{1,65},{65,1},{2,66},{66,2},{3,67},{67,3},{4,68},{68... | collective-permute-start | bytes 3932168 | tf_op jit(solution)/shard_map/ppermute | solution.py:55
  4.7 3.7 %collective-permute-start = (bf16[80,1024]{1,0:T(8,128)(2,1)S(1)}, bf16[80,1024]{1,0:T(8,128)(2,1)S(1)}, u32[]{:S(2)}, u32[]{:S(2)}) collective-permute-start(bf16[80,1024]{1,0:T(8,128)(2,1)S(1)} %get-tuple-element.30), channel_id=1, source_target_pairs={{0,1},{1,2},{2,3},{3,4},{4,5},{5,6},{6,7},{7,8},{8,9},{9,10},{10,1... | collective-permute-start | bytes 491528 | tf_op jit(solution)/shard_map/ppermute | solution.py:59
  8.3 1.3 %collective-permute-start.1 = (bf16[80,1024]{1,0:T(8,128)(2,1)S(1)}, bf16[80,1024]{1,0:T(8,128)(2,1)S(1)}, u32[]{:S(2)}, u32[]{:S(2)}) collective-permute-start(bf16[80,1024]{1,0:T(8,128)(2,1)S(1)} %get-tuple-element.31), channel_id=1, source_target_pairs={{1,0},{2,1},{3,2},{4,3},{5,4},{6,5},{7,6},{8,7},{9,8},{10,9},{11,1... | collective-permute-start | bytes 491528 | tf_op jit(solution)/shard_map/ppermute | solution.py:63
  9.6 0.4 collective-permute-start.3
  10.0 0.9 collective-permute-done.3
  10.9 0.0 collective-permute-done.2.other
  10.9 0.0 copy-done
  10.9 0.0 copy-done.1
  10.9 11.5 %inner.1 = (f32[40,8192]{1,0:T(8,128)S(1)}, f32[40,8192]{1,0:T(8,128)S(1)}, f32[8192,128]{1,0:T(8,128)S(1)}, bf16[12,512,512]{2,1,0:T(8,128)(2,1)S(1)}, bf16[8,512,512]{2,1,0:T(8,128)(2,1)S(1)}) custom-call(f32[40,8192]{1,0:T(8,128)S(1)} %get-tuple-element.28.modes, f32[40,8192]{1,0:T(8,128)S(1)} %get-tuple-element.29.prev, ...), custom_call_target="tpu_custom_call" | custom-call | tf_op jit(solution)/shard_map/inner/pallas_call | solution.py:476
  22.5 0.0 collective-permute-done.left
  22.5 0.0 collective-permute-done.1.right
  22.5 4.5 %outer.1 = (f32[40,8192]{1,0:T(8,128)S(1)}, f32[40,8192]{1,0:T(8,128)S(1)}, f32[1,8192]{1,0:T(1,128)S(1)}, f32[128,128]{1,0:T(8,128)S(1)}) custom-call(f32[40,8192]{1,0:T(8,128)S(1)} %get-tuple-element.28.modes, f32[40,8192]{1,0:T(8,128)S(1)} %get-tuple-element.29.prev, bf16[80,1024]{1,0:T(8,128)(2,1)S(1)} %collective-permute-done.left, ...), custom_call_target="tpu_custom_call" | custom-call | tf_op jit(solution)/shard_map/outer/pallas_call | solution.py:492
  27.0 20.2 %all_to_all.28 = f32[128,1,128]{2,1,0:T(1,128)S(1)} all-to-all(f32[128,1,128]{2,1,0:T(1,128)S(1)} %bitcast.30), channel_id=1, replica_groups=mesh['field'=2,'dom_0'=4,'dom_1'=4,'dom_2'=4] {'field','dom_0','dom_1','..., dimensions={0} | all-to-all | bytes 131072 | tf_op jit(solution)/shard_map/all_to_all | solution.py:67
  47.2 0.4 residual.1
  47.5 0.8 collective-permute-start.6
  48.4 2.4 %collective-permute-start.4 = (bf16[40,1024]{1,0:T(8,128)(2,1)S(1)}, bf16[40,1024]{1,0:T(8,128)(2,1)S(1)}, u32[]{:S(2)}, u32[]{:S(2)}) collective-permute-start(bf16[40,1024]{1,0:T(8,128)(2,1)S(1)} %get-tuple-element.45), channel_id=1, source_target_pairs={{0,1},{1,2},{2,3},{3,4},{4,5},{5,6},{6,7},{7,8},{8,9},{9,10},{10,1... | collective-permute-start | bytes 245768 | tf_op jit(solution)/shard_map/ppermute | solution.py:59
  50.8 1.5 %collective-permute-start.5 = (bf16[40,1024]{1,0:T(8,128)(2,1)S(1)}, bf16[40,1024]{1,0:T(8,128)(2,1)S(1)}, u32[]{:S(2)}, u32[]{:S(2)}) collective-permute-start(bf16[40,1024]{1,0:T(8,128)(2,1)S(1)} %get-tuple-element.46), channel_id=1, source_target_pairs={{1,0},{2,1},{3,2},{4,3},{5,4},{6,5},{7,6},{8,7},{9,8},{10,9},{11,1... | collective-permute-start | bytes 245768 | tf_op jit(solution)/shard_map/ppermute | solution.py:63
  52.3 0.0 collective-permute-done.6.other
  52.3 8.9 %inner_second.1 = (f32[40,8192]{1,0:T(8,128)S(1)}, f32[8192,128]{1,0:T(8,128)S(1)}) custom-call(bf16[40,8192]{1,0:T(8,128)(2,1)S(1)} %get-tuple-element.44.whole, bf16[40,8192]{1,0:T(8,128)(2,1)S(1)} %collective-permute-done.6.other, bf16[12,512,512]{2,1,0:T(8,128)(2,1)S(1)} %get-tuple-element.38.tables, bf16[8,512,512]{2,1,0:T(8,128)(2,1)S(1)} %get-tuple-element.39.flipped, ...), custom_call_target="tpu_custom_call" | custom-call | tf_op jit(solution)/shard_map/inner_second/pallas_call | solution.py:514
  61.2 0.0 collective-permute-done.4.left
  61.2 0.0 collective-permute-done.5.right
  61.2 7.6 %outer_second.1 = (f32[40,8192]{1,0:T(8,128)}, f32[128,128]{1,0:T(8,128)S(1)}) custom-call(f32[40,8192]{1,0:T(8,128)S(1)} %get-tuple-element.43.residual, bf16[40,8192]{1,0:T(8,128)(2,1)S(1)} %get-tuple-element.44.whole, bf16[40,1024]{1,0:T(8,128)(2,1)S(1)} %collective-permute-done.4.left, bf16[40,1024]{1,0:T(8,128)(2,1)S(1)} %collective-permute-done.5.right, ...), custom_call_target="tpu_custom_call" | custom-call | tf_op jit(solution)/shard_map/outer_second/pallas_call | solution.py:526
  68.9 17.8 %all_to_all.29 = f32[128,1,128]{2,1,0:T(1,128)S(1)} all-to-all(f32[128,1,128]{2,1,0:T(1,128)S(1)} %bitcast.29), channel_id=1, replica_groups=mesh['field'=2,'dom_0'=4,'dom_1'=4,'dom_2'=4] {'field','dom_0','dom_1','..., dimensions={0} | all-to-all | bytes 131072 | tf_op jit(solution)/shard_map/all_to_all | solution.py:67
  86.7 0.2 reduce_sum.9
  86.9 13.8 %all_to_all.30 = f32[128,1,128]{2,1,0:T(1,128)S(1)} all-to-all(f32[128,1,128]{2,1,0:T(1,128)S(1)} %broadcast_in_dim.4), channel_id=1, replica_groups=mesh['field'=2,'dom_0'=4,'dom_1'=4,'dom_2'=4] {'field','dom_0','dom_1','..., dimensions={0} | all-to-all | bytes 131072 | tf_op jit(solution)/shard_map/all_to_all | solution.py:67
  100.7 6.5 %final.1 = (f32[120,8192]{1,0:T(8,128)}, f32[120,120]{1,0:T(8,128)}) custom-call(f32[128,128]{1,0:T(8,128)S(1)} %bitcast.19, f32[40,8192]{1,0:T(8,128)S(1)} %get-tuple-element.28.modes, f32[40,8192]{1,0:T(8,128)} %get-tuple-element.51.residual_in, f32[40,8192]{1,0:T(8,128)S(1)} %get-tuple-element.29.prev), custom_call_target="tpu_custom_call" | custom-call | tf_op jit(solution)/shard_map/final/pallas_call | solution.py:546
  (1 shorter events, 0.0 us)
Async XLA Ops:
  1.3 9.6 %copy-start = (s32[1,3,1024]{2,0,1:T(1,128)S(1)}, s32[1,3,1024]{2,0,1:T(1,128)}, u32[]{:S(2)}) copy-start(s32[1,3,1024]{2,0,1:T(1,128)} %param.10) | copy-start | bytes 36868
  1.3 9.6 %copy-start.1 = (f32[1,3,1024]{2,0,1:T(1,128)S(1)}, f32[1,3,1024]{2,0,1:T(1,128)}, u32[]{:S(2)}) copy-start(f32[1,3,1024]{2,0,1:T(1,128)} %param.11) | copy-start | bytes 36868
  3.2 7.7 %collective-permute-start.2 = (bf16[80,8192]{1,0:T(8,128)(2,1)S(1)}, bf16[80,8192]{1,0:T(8,128)(2,1)S(1)}, u32[]{:S(2)}, u32[]{:S(2)}) collective-permute-start(bf16[80,8192]{1,0:T(8,128)(2,1)S(1)} %get-tuple-element.32), channel_id=1, source_target_pairs={{0,64},{64,0},{1,65},{65,1},{2,66},{66,2},{3,67},{67,3},{4,68},{68... | collective-permute-start | bytes 3932168 | tf_op jit(solution)/shard_map/ppermute | solution.py:55
  4.7 17.8 %collective-permute-start = (bf16[80,1024]{1,0:T(8,128)(2,1)S(1)}, bf16[80,1024]{1,0:T(8,128)(2,1)S(1)}, u32[]{:S(2)}, u32[]{:S(2)}) collective-permute-start(bf16[80,1024]{1,0:T(8,128)(2,1)S(1)} %get-tuple-element.30), channel_id=1, source_target_pairs={{0,1},{1,2},{2,3},{3,4},{4,5},{5,6},{6,7},{7,8},{8,9},{9,10},{10,1... | collective-permute-start | bytes 491528 | tf_op jit(solution)/shard_map/ppermute | solution.py:59
  8.3 14.1 %collective-permute-start.1 = (bf16[80,1024]{1,0:T(8,128)(2,1)S(1)}, bf16[80,1024]{1,0:T(8,128)(2,1)S(1)}, u32[]{:S(2)}, u32[]{:S(2)}) collective-permute-start(bf16[80,1024]{1,0:T(8,128)(2,1)S(1)} %get-tuple-element.31), channel_id=1, source_target_pairs={{1,0},{2,1},{3,2},{4,3},{5,4},{6,5},{7,6},{8,7},{9,8},{10,9},{11,1... | collective-permute-start | bytes 491528 | tf_op jit(solution)/shard_map/ppermute | solution.py:63
  9.6 1.3 %collective-permute-start.3 = (s32[24,128]{1,0:T(8,128)S(1)}, s32[24,128]{1,0:T(8,128)S(1)}, u32[]{:S(2)}, u32[]{:S(2)}) collective-permute-start(s32[24,128]{1,0:T(8,128)S(1)} %get-tuple-element.33), channel_id=1, source_target_pairs={{0,64},{64,0},{1,65},{65,1},{2,66},{66,2},{3,67},{67,3},{4,68},{68... | collective-permute-start | bytes 36872 | tf_op jit(solution)/shard_map/ppermute | solution.py:55
  47.5 4.7 %collective-permute-start.6 = (bf16[40,8192]{1,0:T(8,128)(2,1)S(1)}, bf16[40,8192]{1,0:T(8,128)(2,1)S(1)}, u32[]{:S(2)}, u32[]{:S(2)}) collective-permute-start(bf16[40,8192]{1,0:T(8,128)(2,1)S(1)} %get-tuple-element.44.whole), channel_id=1, source_target_pairs={{0,64},{64,0},{1,65},{65,1},{2,66},{66,2},{3,67},{67,3},{4,68},{68... | collective-permute-start | bytes 1966088 | tf_op jit(solution)/shard_map/ppermute | solution.py:55
  48.4 12.9 %collective-permute-start.4 = (bf16[40,1024]{1,0:T(8,128)(2,1)S(1)}, bf16[40,1024]{1,0:T(8,128)(2,1)S(1)}, u32[]{:S(2)}, u32[]{:S(2)}) collective-permute-start(bf16[40,1024]{1,0:T(8,128)(2,1)S(1)} %get-tuple-element.45), channel_id=1, source_target_pairs={{0,1},{1,2},{2,3},{3,4},{4,5},{5,6},{6,7},{7,8},{8,9},{9,10},{10,1... | collective-permute-start | bytes 245768 | tf_op jit(solution)/shard_map/ppermute | solution.py:59
  50.8 10.4 %collective-permute-start.5 = (bf16[40,1024]{1,0:T(8,128)(2,1)S(1)}, bf16[40,1024]{1,0:T(8,128)(2,1)S(1)}, u32[]{:S(2)}, u32[]{:S(2)}) collective-permute-start(bf16[40,1024]{1,0:T(8,128)(2,1)S(1)} %get-tuple-element.46), channel_id=1, source_target_pairs={{1,0},{2,1},{3,2},{4,3},{5,4},{6,5},{7,6},{8,7},{9,8},{10,9},{11,1... | collective-permute-start | bytes 245768 | tf_op jit(solution)/shard_map/ppermute | solution.py:63

commit v2 on v1

--- a/solution.py
+++ b/solution.py
@@ -55,12 +55,17 @@
     return lax.ppermute(value, "field", [(0, 1), (1, 0)])
 
 
-def from_left(value):
-    return lax.ppermute(value, DOM, [(i, i + 1) for i in range(63)])
-
-
-def from_right(value):
-    return lax.ppermute(value, DOM, [(i + 1, i) for i in range(63)])
+def is_even():
+    return lax.rem(lax.axis_index(DOM[2]), 2) == 0
+
+
+def pick(condition, one, two):
+    return jnp.where(condition, one, two)
+
+
+def swap_pairs(value, first):
+    pairs = [(i, i + 1) for i in range(first, 63, 2)]
+    return lax.ppermute(value, DOM, pairs + [(j, i) for i, j in pairs])
 
 
 def exchange(rows):
@@ -69,7 +74,7 @@
 
 def round_kernel(
     modes, prev, coupling, rows, counts,
-    modes_v, prev_v, whole, head, tail, weights, rows_v, sems,
+    modes_v, prev_v, whole, to_near, to_far, weights, rows_v, sems,
 ):
     pairs = ((modes, modes_v), (prev, prev_v), (coupling, weights), (rows, rows_v))
     loads = [
@@ -86,8 +91,10 @@
     weights[...] = jnp.where(slot < counts[0], weights[...], 0.0)
     rounded = jnp.concatenate([modes_v[...], prev_v[...]], axis=0).astype(BF16)
     whole[...] = rounded
-    head[...] = rounded[:, :HALO]
-    tail[...] = rounded[:, ROWS - HALO :]
+    even = is_even()
+    head, tail = rounded[:, :HALO], rounded[:, ROWS - HALO :]
+    to_near[...] = pick(even, tail, head)
+    to_far[...] = pick(even, head, tail)
 
 
 def rounded_parts(modes, prev, coupling, rows, counts):
@@ -109,6 +116,23 @@
     )
 
 
+def fetch(sources, targets, sems):
+    copies = [
+        pltpu.make_async_copy(source, target, sems.at[index])
+        for index, (source, target) in enumerate(zip(sources, targets))
+    ]
+    for copy in copies:
+        copy.start()
+    return copies
+
+
+def scalar_scratch(coupled):
+    kinds = [jnp.int32, F32] + [jnp.int32, jnp.int32, F32] * coupled
+    return [pltpu.SMEM((IFACE,), kind) for kind in kinds] + [
+        pltpu.SemaphoreType.DMA((len(kinds),))
+    ]
+
+
 def block_sum(b, at, blocks, tables, flipped, kinds, scales, beside=None):
     first = domain_index() * NBR
     total = None
@@ -146,9 +170,12 @@
 
 
 def inner_kernel(
-    modes, prev, other, tables_in, kinds, scales, rows, rows_o, weights,
-    partial_x, partial_p, coup, tables, flipped, blocks, other_t, sems,
+    modes, prev, other, tables_in, *refs
 ):
+    scalars, refs = refs[:5], refs[5:]
+    partial_x, partial_p, coup, tables, flipped, blocks, other_t, sems = refs[:8]
+    kinds, scales, rows, rows_o, weights, scalar_sems = refs[8:]
+    fetched = fetch(scalars, (kinds, scales, rows, rows_o, weights), scalar_sems)
     loads = [
         pltpu.make_async_copy(
             tables_in.at[pl.ds(offset * NTYPE, NTYPE)],
@@ -171,6 +198,8 @@
         for index in range(NTYPE):
             flipped[(offset - 1) * NTYPE + index] = tables[offset * NTYPE + index].T
     loads[0].wait()
+    for copy in fetched:
+        copy.wait()
     steps = (NBR - 4) // INNER
     slots = IFACE // steps
 
@@ -188,17 +217,22 @@
 
 
 def outer_kernel(
-    modes, prev, left, right, partial_x, partial_p, coup, tables, flipped, kinds, scales,
-    image_x, image_p, inverse_j, sums, ends,
+    modes, prev, near, far, partial_x, partial_p, coup, tables, flipped, kinds_in, scales_in,
+    image_x, image_p, inverse_j, sums, ends, kinds, scales, scalar_sems,
 ):
+    fetched = fetch((kinds_in, scales_in), (kinds, scales), scalar_sems)
     first = domain_index() * NBR
+    even = is_even()
     for b in range(2):
         span = slice(b * BS, (b + 1) * BS)
-        ends[b] = left[:, span]
-        ends[10 + b] = right[:, span]
+        ends[b] = pick(even, far[:, span], near[:, span])
+        ends[10 + b] = pick(even, near[:, span], far[:, span])
     for at, b in ENDS:
         span = slice(b * BS, (b + 1) * BS)
         ends[at] = jnp.concatenate([modes[:, span], prev[:, span]], axis=0).astype(BF16)
+
+    for copy in fetched:
+        copy.wait()
 
     def step(index, carry):
         for u in range(2):
@@ -248,7 +282,7 @@
     sums[...] = jnp.broadcast_to(total, (ALL_DEV, LANES))
 
 
-def residual_kernel(gathered, modes, image_x, inverse_j, residual, whole, head, tail):
+def residual_kernel(gathered, modes, image_x, inverse_j, residual, whole, to_near, to_far):
     total = jnp.sum(gathered[...], axis=0, keepdims=True)
     column = jnp.broadcast_to(total, (LANES, LANES)).T
     quotient = column[MODES:PAIR, :] / column[:MODES, :]
@@ -256,25 +290,27 @@
         span = slice(c * LANES, (c + 1) * LANES)
         value = (image_x[:, span] - modes[:, span] * quotient) * inverse_j[:, span]
         residual[:, span] = value
-        low = value.astype(BF16)
-        whole[:, span] = low
-        if c < HALO // LANES:
-            head[:, span] = low
-        if c >= TILES - HALO // LANES:
-            at = (c - (TILES - HALO // LANES)) * LANES
-            tail[:, at : at + LANES] = low
+        whole[:, span] = value.astype(BF16)
+    even = is_even()
+    head, tail = whole[:, :HALO], whole[:, ROWS - HALO :]
+    to_near[...] = pick(even, tail, head)
+    to_far[...] = pick(even, head, tail)
 
 
 def inner_second_kernel(
-    whole, other, tables, flipped, kinds, scales, rows, rows_o, weights,
-    partial, coup, blocks, other_t,
+    whole, other, tables, flipped, *refs
 ):
+    scalars, refs = refs[:5], refs[5:]
+    partial, coup, blocks, other_t, kinds, scales, rows, rows_o, weights, scalar_sems = refs
+    fetched = fetch(scalars, (kinds, scales, rows, rows_o, weights), scalar_sems)
     for b in range(NBR):
         blocks[b, :MODES] = whole[:, b * BS : (b + 1) * BS]
     for c in range(TILES):
         span = slice(c * LANES, (c + 1) * LANES)
         other_t[span, :MODES] = other[:, span].astype(F32).T
     coup[...] = jnp.zeros_like(coup)
+    for copy in fetched:
+        copy.wait()
     steps = (NBR - 4) // INNER
     slots = IFACE // steps
 
@@ -290,18 +326,24 @@
 
 
 def outer_second_kernel(
-    residual, whole, left, right, partial, coup, tables, flipped, kinds, scales,
+    residual, whole, near, far, partial, coup, tables, flipped, kinds_in, scales_in,
     modes, prev, image_x, image_p, residual_out, packed, ends, image_e, gram, sem,
+    kinds, scales, scalar_sems,
 ):
-    copy = pltpu.make_async_copy(residual, residual_out, sem)
-    copy.start()
+    fetched = fetch((kinds_in, scales_in), (kinds, scales), scalar_sems)
+    even = is_even()
+    stored = pltpu.make_async_copy(residual, residual_out, sem)
+    stored.start()
     for b in range(2):
         span = slice(b * BS, (b + 1) * BS)
-        ends[b, :MODES] = left[:, span]
-        ends[10 + b, :MODES] = right[:, span]
+        ends[b, :MODES] = pick(even, far[:, span], near[:, span])
+        ends[10 + b, :MODES] = pick(even, near[:, span], far[:, span])
     for at, b in ENDS:
         ends[at, :MODES] = whole[:, b * BS : (b + 1) * BS]
     gram[...] = jnp.zeros_like(gram)
+
+    for copy in fetched:
+        copy.wait()
 
     def blocked(index, carry):
         for u in range(2):
@@ -356,7 +398,7 @@
     diagonal = jnp.sum(jnp.where(row == col, gram_a, 0.0), axis=0, keepdims=True)
     merged = jnp.where(row >= col, gram_b, gram_a)
     packed[...] = jnp.where(row == n, jnp.broadcast_to(diagonal, (LANES, LANES)), merged)
-    copy.wait()
+    stored.wait()
 
 
 def lower_inverse(gram, count):
@@ -419,18 +461,9 @@
     gram_a = jnp.where(row == col, diagonal, gram_a) / (2.0 * ndof)
     gram_a = jnp.where(inside, gram_a, 0.0)
     factors = jnp.concatenate(lower_inverse(gram_b, n), axis=0)
-    half = lax.dot_general(
-        factors, gram_a, (((1,), (0,)), ((), ())),
-        precision=lax.Precision.HIGHEST, preferred_element_type=F32,
-    )
-    whole = lax.dot_general(
-        half, factors, (((1,), (1,)), ((), ())),
-        precision=lax.Precision.HIGHEST, preferred_element_type=F32,
-    )
-    projected[...] = whole
-    factors = factors[:, :n]
-    high = factors.astype(BF16)
-    low = (factors - high.astype(F32)).astype(BF16)
+    square = factors[:, :n]
+    high = square.astype(BF16)
+    low = (square - high.astype(F32)).astype(BF16)
     top = jnp.concatenate([high, high], axis=1)
     dims = (((1,), (0,)), ((), ()))
     load.wait()
@@ -449,6 +482,15 @@
         )
         store.start()
         stores.append(store)
+    half = lax.dot_general(
+        factors, gram_a, (((1,), (0,)), ((), ())),
+        precision=lax.Precision.HIGHEST, preferred_element_type=F32,
+    )
+    whole = lax.dot_general(
+        half, factors, (((1,), (1,)), ((), ())),
+        precision=lax.Precision.HIGHEST, preferred_element_type=F32,
+    )
+    projected[...] = whole
     for store in stores:
         store.wait()
 
@@ -460,15 +502,15 @@
     scales = scales[0].reshape(3 * NBLK)
     tables = tables[0].reshape(3 * NTYPE, BS, BS)
     rows = wet_rows[0]
-    modes, prev, whole, head, tail, weights, rows = rounded_parts(
+    modes, prev, whole, to_near, to_far, weights, rows = rounded_parts(
         modes, prev, coupling, rows, wet_counts
     )
     weights = weights.reshape(IFACE)
     rows_o = swap_field(rows).reshape(IFACE)
     rows = rows.reshape(IFACE)
     other = swap_field(whole)
-    left = from_left(tail)
-    right = from_right(head)
+    near = swap_pairs(to_near, 0)
+    far = swap_pairs(to_far, 1)
     coupling_args = (rows, rows_o, weights)
     plane = shape(MODES, ROWS)
     rows_by_lanes = shape(ROWS, LANES)
@@ -479,12 +521,13 @@
             plane, plane, rows_by_lanes,
             shape(3 * NTYPE, BS, BS, kind=BF16), shape(2 * NTYPE, BS, BS, kind=BF16),
         ),
-        in_specs=[VMEM] * 3 + [HBM] + [SMEM] * 5,
+        in_specs=[VMEM] * 3 + [HBM] + [VMEM] * 5,
         out_specs=[VMEM] * 5,
         scratch_shapes=[
             pltpu.VMEM((NBR, PAIR, BS), BF16),
             pltpu.VMEM((ROWS, LANES), F32),
             pltpu.SemaphoreType.DMA((3,)),
+            *scalar_scratch(True),
         ],
         compiler_params=params(10),
         name="inner",
@@ -492,15 +535,15 @@
     image_x, image_p, inverse_j, sums = pl.pallas_call(
         outer_kernel,
         out_shape=(plane, plane, shape(1, ROWS), shape(ALL_DEV, LANES)),
-        in_specs=[VMEM] * 9 + [SMEM] * 2,
+        in_specs=[VMEM] * 11,
         out_specs=[VMEM] * 4,
-        scratch_shapes=[pltpu.VMEM((12, PAIR, BS), BF16)],
+        scratch_shapes=[pltpu.VMEM((12, PAIR, BS), BF16), *scalar_scratch(False)],
         compiler_params=params(6),
         name="outer",
-    )(modes, prev, left, right, partial_x, partial_p, coup, tables, flipped, kinds, scales)
+    )(modes, prev, near, far, partial_x, partial_p, coup, tables, flipped, kinds, scales)
     gathered = exchange(sums)
     end = shape(MODES, HALO, kind=BF16)
-    residual, whole, head, tail = pl.pallas_call(
+    residual, whole, to_near, to_far = pl.pallas_call(
         residual_kernel,
         out_shape=(plane, shape(MODES, ROWS, kind=BF16), end, end),
         in_specs=[VMEM] * 4,
@@ -509,16 +552,17 @@
         name="residual",
     )(gathered, modes, image_x, inverse_j)
     other = swap_field(whole)
-    left = from_left(tail)
-    right = from_right(head)
+    near = swap_pairs(to_near, 0)
+    far = swap_pairs(to_far, 1)
     partial, coup = pl.pallas_call(
         inner_second_kernel,
         out_shape=(plane, rows_by_lanes),
-        in_specs=[VMEM] * 4 + [SMEM] * 5,
+        in_specs=[VMEM] * 9,
         out_specs=[VMEM] * 2,
         scratch_shapes=[
             pltpu.VMEM((NBR, SINGLE, BS), BF16),
             pltpu.VMEM((ROWS, LANES), F32),
+            *scalar_scratch(True),
         ],
         compiler_params=params(10),
         name="inner_second",
@@ -526,18 +570,19 @@
     residual, packed = pl.pallas_call(
         outer_second_kernel,
         out_shape=(pltpu.HBM((MODES, ROWS), F32), shape(LANES, LANES)),
-        in_specs=[VMEM] * 8 + [SMEM] * 2 + [VMEM] * 4,
+        in_specs=[VMEM] * 14,
         out_specs=[HBM, VMEM],
         scratch_shapes=[
             pltpu.VMEM((12, SINGLE, BS), BF16),
             pltpu.VMEM((MODES, 4 * BS), F32),
             pltpu.VMEM((12 * MODES, 6 * MODES), F32),
             pltpu.SemaphoreType.DMA(()),
+            *scalar_scratch(False),
         ],
         compiler_params=params(10),
         name="outer_second",
     )(
-        residual, whole, left, right, partial, coup, tables, flipped, kinds, scales,
+        residual, whole, near, far, partial, coup, tables, flipped, kinds, scales,
         modes, prev, image_x, image_p,
     )
     part = jnp.sum(exchange(packed), axis=0, keepdims=True)

time: 108 us -> 101 us (0.935)
  starting transfers between devices: 11.5 us -> 6.52 us
  Pallas kernels: 41.3 us -> 38.2 us
    ppermute x4, starting transfers between devices: 8.86 us -> 3.8 us  [swap_pairs(): return lax.ppermute(value, DOM, pairs + [(j, i) for i, j in pairs])]
    pallas_call x1, Pallas kernels: 11.5 us -> 10.2 us  [shards(): pl.pallas_call(inner_kernel, out_shape=(plane, plane, rows_by_lanes, shap...]
  transfers between devices with their start and end apart: 7 -> 7, of which waited for: 1 -> 2; matrix products, arithmetic and copies ran while one was open for 0% -> 0% of each run, Pallas kernels for 19% -> 18%
where the time goes in v2:
time: 101 us; the launch traced here: 100 us
  blocking collectives  52.6 us (52%)
  Pallas kernels  38.2 us (38%)
  starting transfers between devices  6.52 us (6%)
  between operations  1.56 us (2%)
  waiting for transfers between devices  1.18 us (1%)
    all_to_all x3, blocking collectives, exchange(): return lax.all_to_all(rows, FIELD_DOM, 0, 0, tiled=True)  52.6 us
    pallas_call x1, Pallas kernels, shards(): pl.pallas_call(inner_kernel, out_shape=(plane, plane, rows_by_lanes, shap...  10.2 us
    pallas_call x1, Pallas kernels, shards(): pl.pallas_call(inner_second_kernel, out_shape=(plane, rows_by_lanes), in_...  8.06 us
    pallas_call x1, Pallas kernels, shards(): pl.pallas_call(outer_second_kernel, out_shape=(pltpu.HBM((MODES, ROWS), F...  7.57 us
    pallas_call x1, Pallas kernels, shards(): pl.pallas_call(final_kernel, out_shape=(pltpu.HBM((n, ROWS), F32), shape(...  5.72 us
    pallas_call x1, Pallas kernels, shards(): pl.pallas_call(outer_kernel, out_shape=(plane, plane, shape(1, ROWS), sha...  4.47 us
    ppermute x4, starting transfers between devices, swap_pairs(): return lax.ppermute(value, DOM, pairs + [(j, i) for i, j in pairs])  3.8 us
    ppermute x3, starting transfers between devices, swap_field(): return lax.ppermute(value, 'field', [(0, 1), (1, 0)])  2.72 us
  transfers between devices with their start and end apart: 7, of which 2 were waited for; matrix products, arithmetic and copies ran while one was open for 0% of the time, Pallas kernels for 18%

profile of v2, /device:TPU:1, one launch (start us, length us, event | category | flops | bytes accessed | tf_op | source)
XLA Modules:
  0.0 100.3 jit_solution(7045774017796776063)
XLA Ops:
  1.3 0.0 copy-start
  1.3 0.0 copy-start.1
  1.3 1.9 %rounded.1 = (f32[40,8192]{1,0:T(8,128)S(1)}, f32[40,8192]{1,0:T(8,128)S(1)}, bf16[80,8192]{1,0:T(8,128)(2,1)S(1)}, bf16[80,1024]{1,0:T(8,128)(2,1)S(1)}, bf16[8...) custom-call(f32[40,8192]{1,0:T(8,128)} %bitcast.38, f32[40,8192]{1,0:T(8,128)} %bitcast.39, ...), custom_call_target="tpu_custom_call" | custom-call | tf_op jit(solution)/shard_map/rounded/pallas_call | solution.py:104
  3.2 1.5 %collective-permute-start.2 = (bf16[80,8192]{1,0:T(8,128)(2,1)S(1)}, bf16[80,8192]{1,0:T(8,128)(2,1)S(1)}, u32[]{:S(2)}, u32[]{:S(2)}) collective-permute-start(bf16[80,8192]{1,0:T(8,128)(2,1)S(1)} %get-tuple-element.32), channel_id=1, source_target_pairs={{0,64},{64,0},{1,65},{65,1},{2,66},{66,2},{3,67},{67,3},{4,68},{68... | collective-permute-start | bytes 3932168 | tf_op jit(solution)/shard_map/ppermute | solution.py:55
  4.7 1.7 %collective-permute-start = (bf16[80,1024]{1,0:T(8,128)(2,1)S(1)}, bf16[80,1024]{1,0:T(8,128)(2,1)S(1)}, u32[]{:S(2)}, u32[]{:S(2)}) collective-permute-start(bf16[80,1024]{1,0:T(8,128)(2,1)S(1)} %get-tuple-element.30), channel_id=1, source_target_pairs={{0,1},{2,3},{4,5},{6,7},{8,9},{10,11},{12,13},{14,15},{16,17},{18,... | collective-permute-start | bytes 491528 | tf_op jit(solution)/shard_map/ppermute | solution.py:68
  6.4 0.7 collective-permute-start.1
  7.1 0.5 collective-permute-start.3
  7.5 0.8 collective-permute-done.3
  8.4 0.0 collective-permute-done.2.other
  8.4 0.0 copy-done
  8.4 0.0 copy-done.1
  8.4 10.2 %inner.1 = (f32[40,8192]{1,0:T(8,128)S(1)}, f32[40,8192]{1,0:T(8,128)S(1)}, f32[8192,128]{1,0:T(8,128)S(1)}, bf16[12,512,512]{2,1,0:T(8,128)(2,1)S(1)}, bf16[8,512,512]{2,1,0:T(8,128)(2,1)S(1)}) custom-call(f32[40,8192]{1,0:T(8,128)S(1)} %get-tuple-element.28.modes, f32[40,8192]{1,0:T(8,128)S(1)} %get-tuple-element.29.prev, ...), custom_call_target="tpu_custom_call" | custom-call | tf_op jit(solution)/shard_map/inner/pallas_call | solution.py:518
  18.6 0.0 collective-permute-done.near
  18.6 0.0 collective-permute-done.1.far
  18.6 4.5 %outer.1 = (f32[40,8192]{1,0:T(8,128)S(1)}, f32[40,8192]{1,0:T(8,128)S(1)}, f32[1,8192]{1,0:T(1,128)S(1)}, f32[128,128]{1,0:T(8,128)S(1)}) custom-call(f32[40,8192]{1,0:T(8,128)S(1)} %get-tuple-element.28.modes, f32[40,8192]{1,0:T(8,128)S(1)} %get-tuple-element.29.prev, bf16[80,1024]{1,0:T(8,128)(2,1)S(1)} %collective-permute-done.near, ...), custom_call_target="tpu_custom_call" | custom-call | tf_op jit(solution)/shard_map/outer/pallas_call | solution.py:535
  23.0 20.7 %all_to_all.28 = f32[128,1,128]{2,1,0:T(1,128)S(1)} all-to-all(f32[128,1,128]{2,1,0:T(1,128)S(1)} %bitcast.30), channel_id=1, replica_groups=mesh['field'=2,'dom_0'=4,'dom_1'=4,'dom_2'=4] {'field','dom_0','dom_1','..., dimensions={0} | all-to-all | bytes 131072 | tf_op jit(solution)/shard_map/all_to_all | solution.py:72
  43.7 0.4 residual.1
  44.1 0.8 collective-permute-start.6
  44.9 0.6 collective-permute-start.4
  45.5 0.8 collective-permute-start.5
  46.3 0.3 collective-permute-done.6.other
  46.6 8.1 %inner_second.1 = (f32[40,8192]{1,0:T(8,128)S(1)}, f32[8192,128]{1,0:T(8,128)S(1)}) custom-call(bf16[40,8192]{1,0:T(8,128)(2,1)S(1)} %get-tuple-element.44.whole, bf16[40,8192]{1,0:T(8,128)(2,1)S(1)} %collective-permute-done.6.other, bf16[12,512,512]{2,1,0:T(8,128)(2,1)S(1)} %get-tuple-element.38.tables, bf16[8,512,512]{2,1,0:T(8,128)(2,1)S(1)} %get-tuple-element.39.flipped, ...), custom_call_target="tpu_custom_call" | custom-call | tf_op jit(solution)/shard_map/inner_second/pallas_call | solution.py:557
  54.7 0.0 collective-permute-done.4.near
  54.7 0.0 collective-permute-done.5.far
  54.7 7.6 %outer_second.1 = (f32[40,8192]{1,0:T(8,128)}, f32[128,128]{1,0:T(8,128)S(1)}) custom-call(f32[40,8192]{1,0:T(8,128)S(1)} %get-tuple-element.43.residual, bf16[40,8192]{1,0:T(8,128)(2,1)S(1)} %get-tuple-element.44.whole, bf16[40,1024]{1,0:T(8,128)(2,1)S(1)} %collective-permute-done.4.near, bf16[40,1024]{1,0:T(8,128)(2,1)S(1)} %collective-permute-done.5.far, ...), custom_call_target="tpu_custom_call" | custom-call | tf_op jit(solution)/shard_map/outer_second/pallas_call | solution.py:570
  62.3 18.1 %all_to_all.29 = f32[128,1,128]{2,1,0:T(1,128)S(1)} all-to-all(f32[128,1,128]{2,1,0:T(1,128)S(1)} %bitcast.29), channel_id=1, replica_groups=mesh['field'=2,'dom_0'=4,'dom_1'=4,'dom_2'=4] {'field','dom_0','dom_1','..., dimensions={0} | all-to-all | bytes 131072 | tf_op jit(solution)/shard_map/all_to_all | solution.py:72
  80.4 0.2 reduce_sum.9
  80.6 13.8 %all_to_all.30 = f32[128,1,128]{2,1,0:T(1,128)S(1)} all-to-all(f32[128,1,128]{2,1,0:T(1,128)S(1)} %broadcast_in_dim.4), channel_id=1, replica_groups=mesh['field'=2,'dom_0'=4,'dom_1'=4,'dom_2'=4] {'field','dom_0','dom_1','..., dimensions={0} | all-to-all | bytes 131072 | tf_op jit(solution)/shard_map/all_to_all | solution.py:72
  94.4 5.7 %final.1 = (f32[120,8192]{1,0:T(8,128)}, f32[120,120]{1,0:T(8,128)}) custom-call(f32[128,128]{1,0:T(8,128)S(1)} %bitcast.19, f32[40,8192]{1,0:T(8,128)S(1)} %get-tuple-element.28.modes, f32[40,8192]{1,0:T(8,128)} %get-tuple-element.51.residual_in, f32[40,8192]{1,0:T(8,128)S(1)} %get-tuple-element.29.prev), custom_call_target="tpu_custom_call" | custom-call | tf_op jit(solution)/shard_map/final/pallas_call | solution.py:591
  (1 shorter events, 0.0 us)
Async XLA Ops:
  1.3 7.1 %copy-start = (s32[1,3,1024]{2,0,1:T(1,128)S(1)}, s32[1,3,1024]{2,0,1:T(1,128)}, u32[]{:S(2)}) copy-start(s32[1,3,1024]{2,0,1:T(1,128)} %param.10) | copy-start | bytes 36868
  1.3 7.1 %copy-start.1 = (f32[1,3,1024]{2,0,1:T(1,128)S(1)}, f32[1,3,1024]{2,0,1:T(1,128)}, u32[]{:S(2)}) copy-start(f32[1,3,1024]{2,0,1:T(1,128)} %param.11) | copy-start | bytes 36868
  3.2 5.2 %collective-permute-start.2 = (bf16[80,8192]{1,0:T(8,128)(2,1)S(1)}, bf16[80,8192]{1,0:T(8,128)(2,1)S(1)}, u32[]{:S(2)}, u32[]{:S(2)}) collective-permute-start(bf16[80,8192]{1,0:T(8,128)(2,1)S(1)} %get-tuple-element.32), channel_id=1, source_target_pairs={{0,64},{64,0},{1,65},{65,1},{2,66},{66,2},{3,67},{67,3},{4,68},{68... | collective-permute-start | bytes 3932168 | tf_op jit(solution)/shard_map/ppermute | solution.py:55
  4.7 13.9 %collective-permute-start = (bf16[80,1024]{1,0:T(8,128)(2,1)S(1)}, bf16[80,1024]{1,0:T(8,128)(2,1)S(1)}, u32[]{:S(2)}, u32[]{:S(2)}) collective-permute-start(bf16[80,1024]{1,0:T(8,128)(2,1)S(1)} %get-tuple-element.30), channel_id=1, source_target_pairs={{0,1},{2,3},{4,5},{6,7},{8,9},{10,11},{12,13},{14,15},{16,17},{18,... | collective-permute-start | bytes 491528 | tf_op jit(solution)/shard_map/ppermute | solution.py:68
  6.4 12.1 %collective-permute-start.1 = (bf16[80,1024]{1,0:T(8,128)(2,1)S(1)}, bf16[80,1024]{1,0:T(8,128)(2,1)S(1)}, u32[]{:S(2)}, u32[]{:S(2)}) collective-permute-start(bf16[80,1024]{1,0:T(8,128)(2,1)S(1)} %get-tuple-element.31), channel_id=1, source_target_pairs={{1,2},{3,4},{5,6},{7,8},{9,10},{11,12},{13,14},{15,16},{17,18},{19... | collective-permute-start | bytes 491528 | tf_op jit(solution)/shard_map/ppermute | solution.py:68
  7.1 1.3 %collective-permute-start.3 = (s32[24,128]{1,0:T(8,128)S(1)}, s32[24,128]{1,0:T(8,128)S(1)}, u32[]{:S(2)}, u32[]{:S(2)}) collective-permute-start(s32[24,128]{1,0:T(8,128)S(1)} %get-tuple-element.33), channel_id=1, source_target_pairs={{0,64},{64,0},{1,65},{65,1},{2,66},{66,2},{3,67},{67,3},{4,68},{68... | collective-permute-start | bytes 36872 | tf_op jit(solution)/shard_map/ppermute | solution.py:55
  44.1 2.5 %collective-permute-start.6 = (bf16[40,8192]{1,0:T(8,128)(2,1)S(1)}, bf16[40,8192]{1,0:T(8,128)(2,1)S(1)}, u32[]{:S(2)}, u32[]{:S(2)}) collective-permute-start(bf16[40,8192]{1,0:T(8,128)(2,1)S(1)} %get-tuple-element.44.whole), channel_id=1, source_target_pairs={{0,64},{64,0},{1,65},{65,1},{2,66},{66,2},{3,67},{67,3},{4,68},{68... | collective-permute-start | bytes 1966088 | tf_op jit(solution)/shard_map/ppermute | solution.py:55
  44.9 9.8 %collective-permute-start.4 = (bf16[40,1024]{1,0:T(8,128)(2,1)S(1)}, bf16[40,1024]{1,0:T(8,128)(2,1)S(1)}, u32[]{:S(2)}, u32[]{:S(2)}) collective-permute-start(bf16[40,1024]{1,0:T(8,128)(2,1)S(1)} %get-tuple-element.45), channel_id=1, source_target_pairs={{0,1},{2,3},{4,5},{6,7},{8,9},{10,11},{12,13},{14,15},{16,17},{18,... | collective-permute-start | bytes 245768 | tf_op jit(solution)/shard_map/ppermute | solution.py:68
  45.5 9.2 %collective-permute-start.5 = (bf16[40,1024]{1,0:T(8,128)(2,1)S(1)}, bf16[40,1024]{1,0:T(8,128)(2,1)S(1)}, u32[]{:S(2)}, u32[]{:S(2)}) collective-permute-start(bf16[40,1024]{1,0:T(8,128)(2,1)S(1)} %get-tuple-element.46), channel_id=1, source_target_pairs={{1,2},{3,4},{5,6},{7,8},{9,10},{11,12},{13,14},{15,16},{17,18},{19... | collective-permute-start | bytes 245768 | tf_op jit(solution)/shard_map/ppermute | solution.py:68

commit v3 on v2

--- a/solution.py
+++ b/solution.py
@@ -241,9 +241,24 @@
             span = pl.ds(pl.multiple_of(b * BS, BS), BS)
             image_x[:, span] = total[:MODES]
             image_p[:, span] = total[MODES:]
+        tiles = (TILES - 4 * BS // LANES) // 2
+        for v in range(tiles):
+            at = 2 * BS + (index * tiles + v) * LANES
+            span = pl.ds(pl.multiple_of(at, LANES), LANES)
+            carry = finish(span, partial_x, partial_p, carry)
         return carry
 
-    lax.fori_loop(0, 2, step, 0)
+    def finish(span, source_x, source_p, carry):
+        squares, crossed = carry
+        coupled = coup[span, :].T
+        value = source_x[:, span] + coupled[:MODES]
+        image_x[:, span] = value
+        image_p[:, span] = source_p[:, span] + coupled[MODES:PAIR]
+        own = modes[:, span]
+        return squares + own * own, crossed + own * value
+
+    nothing = jnp.zeros((MODES, LANES), F32)
+    carry = lax.fori_loop(0, 2, step, (nothing, nothing))
     on_diagonal = lax.broadcasted_iota(jnp.int32, (LANES, LANES), 0) == lax.broadcasted_iota(
         jnp.int32, (LANES, LANES), 1
     )
@@ -259,24 +274,17 @@
                 for kind in range(NTYPE)
             ]
         )
-    squares = jnp.zeros((MODES, LANES), F32)
-    crossed = jnp.zeros((MODES, LANES), F32)
     for c in range(TILES):
         b, part = divmod(c, BS // LANES)
         span = slice(c * LANES, (c + 1) * LANES)
-        coupled = coup[span, :].T
-        source_x, source_p = (partial_x, partial_p) if 2 <= b < NBR - 2 else (image_x, image_p)
-        value = source_x[:, span] + coupled[:MODES]
-        image_x[:, span] = value
-        image_p[:, span] = source_p[:, span] + coupled[MODES:PAIR]
-        own = modes[:, span]
-        squares += own * own
-        crossed += own * value
+        if not 2 <= b < NBR - 2:
+            carry = finish(span, image_x, image_p, carry)
         kind = kinds[first + b]
         line = lines[part][0]
         for other_kind in range(1, NTYPE):
             line = jnp.where(kind == other_kind, lines[part][other_kind], line)
         inverse_j[:, span] = 1.0 / (scales[first + b] * line)
+    squares, crossed = carry
     both = jnp.concatenate([squares, crossed, jnp.zeros((LANES - PAIR, LANES), F32)], axis=0)
     total = jnp.sum(both.T, axis=0, keepdims=True)
     sums[...] = jnp.broadcast_to(total, (ALL_DEV, LANES))
@@ -298,8 +306,9 @@
 
 
 def inner_second_kernel(
-    whole, other, tables, flipped, *refs
+    coupled, whole, other, tables, flipped, *refs
 ):
+    del coupled
     scalars, refs = refs[:5], refs[5:]
     partial, coup, blocks, other_t, kinds, scales, rows, rows_o, weights, scalar_sems = refs
     fetched = fetch(scalars, (kinds, scales, rows, rows_o, weights), scalar_sems)
@@ -308,7 +317,6 @@
     for c in range(TILES):
         span = slice(c * LANES, (c + 1) * LANES)
         other_t[span, :MODES] = other[:, span].astype(F32).T
-    coup[...] = jnp.zeros_like(coup)
     for copy in fetched:
         copy.wait()
     steps = (NBR - 4) // INNER
@@ -371,13 +379,15 @@
             preferred_element_type=F32,
         )
 
-    def step(b, carry):
-        add(b, partial[:, pl.ds(pl.multiple_of(b * 2 * BS, 2 * BS), 2 * BS)])
+    def step(index, carry):
+        for u in range(3):
+            b = 1 + index * 3 + u
+            add(b, partial[:, pl.ds(pl.multiple_of(b * 2 * BS, 2 * BS), 2 * BS)])
         return carry
 
     last = NBR // 2 - 1
+    lax.fori_loop(0, last // 3, step, 0)
     add(0, image_e[:, : 2 * BS])
-    lax.fori_loop(1, last, step, 0)
     add(last, image_e[:, 2 * BS :])
     n = 3 * MODES
     pad = LANES - n
@@ -557,8 +567,9 @@
     partial, coup = pl.pallas_call(
         inner_second_kernel,
         out_shape=(plane, rows_by_lanes),
-        in_specs=[VMEM] * 9,
+        in_specs=[VMEM] * 10,
         out_specs=[VMEM] * 2,
+        input_output_aliases={0: 1},
         scratch_shapes=[
             pltpu.VMEM((NBR, SINGLE, BS), BF16),
             pltpu.VMEM((ROWS, LANES), F32),
@@ -566,7 +577,7 @@
         ],
         compiler_params=params(10),
         name="inner_second",
-    )(whole, other, tables, flipped, kinds, scales, *coupling_args)
+    )(coup, whole, other, tables, flipped, kinds, scales, *coupling_args)
     residual, packed = pl.pallas_call(
         outer_second_kernel,
         out_shape=(pltpu.HBM((MODES, ROWS), F32), shape(LANES, LANES)),

time: 101 us -> 98.8 us (0.978)
  Pallas kernels: 38.2 us -> 36.5 us
    pallas_call x1, Pallas kernels: 7.57 us -> 6.29 us  [shards(): pl.pallas_call(outer_second_kernel, out_shape=(pltpu.HBM((MODES, ROWS), F...]
where the time goes in v3:
time: 98.8 us; the launch traced here: 98.6 us
  blocking collectives  52.6 us (53%)
  Pallas kernels  36.5 us (37%)
  starting transfers between devices  6.52 us (7%)
  between operations  1.56 us (2%)
  waiting for transfers between devices  1.18 us (1%)
    all_to_all x3, blocking collectives, exchange(): return lax.all_to_all(rows, FIELD_DOM, 0, 0, tiled=True)  52.6 us
    pallas_call x1, Pallas kernels, shards(): pl.pallas_call(inner_kernel, out_shape=(plane, plane, rows_by_lanes, shap...  10.2 us
    pallas_call x1, Pallas kernels, shards(): pl.pallas_call(inner_second_kernel, out_shape=(plane, rows_by_lanes), in_...  8.05 us
    pallas_call x1, Pallas kernels, shards(): pl.pallas_call(outer_second_kernel, out_shape=(pltpu.HBM((MODES, ROWS), F...  6.29 us
    pallas_call x1, Pallas kernels, shards(): pl.pallas_call(final_kernel, out_shape=(pltpu.HBM((n, ROWS), F32), shape(...  5.72 us
    pallas_call x1, Pallas kernels, shards(): pl.pallas_call(outer_kernel, out_shape=(plane, plane, shape(1, ROWS), sha...  4.03 us
    ppermute x4, starting transfers between devices, swap_pairs(): return lax.ppermute(value, DOM, pairs + [(j, i) for i, j in pairs])  3.8 us
    ppermute x3, starting transfers between devices, swap_field(): return lax.ppermute(value, 'field', [(0, 1), (1, 0)])  2.72 us
  transfers between devices with their start and end apart: 7, of which 2 were waited for; matrix products, arithmetic and copies ran while one was open for 0% of the time, Pallas kernels for 18%

profile of v3, /device:TPU:1, one launch (start us, length us, event | category | flops | bytes accessed | tf_op | source)
XLA Modules:
  0.0 98.6 jit_solution(11848715018367945040)
XLA Ops:
  1.3 0.0 copy-start
  1.3 0.0 copy-start.1
  1.3 1.9 %rounded.1 = (f32[40,8192]{1,0:T(8,128)S(1)}, f32[40,8192]{1,0:T(8,128)S(1)}, bf16[80,8192]{1,0:T(8,128)(2,1)S(1)}, bf16[80,1024]{1,0:T(8,128)(2,1)S(1)}, bf16[8...) custom-call(f32[40,8192]{1,0:T(8,128)} %bitcast.38, f32[40,8192]{1,0:T(8,128)} %bitcast.39, ...), custom_call_target="tpu_custom_call" | custom-call | tf_op jit(solution)/shard_map/rounded/pallas_call | solution.py:104
  3.2 1.5 %collective-permute-start.2 = (bf16[80,8192]{1,0:T(8,128)(2,1)S(1)}, bf16[80,8192]{1,0:T(8,128)(2,1)S(1)}, u32[]{:S(2)}, u32[]{:S(2)}) collective-permute-start(bf16[80,8192]{1,0:T(8,128)(2,1)S(1)} %get-tuple-element.32), channel_id=1, source_target_pairs={{0,64},{64,0},{1,65},{65,1},{2,66},{66,2},{3,67},{67,3},{4,68},{68... | collective-permute-start | bytes 3932168 | tf_op jit(solution)/shard_map/ppermute | solution.py:55
  4.7 1.7 %collective-permute-start = (bf16[80,1024]{1,0:T(8,128)(2,1)S(1)}, bf16[80,1024]{1,0:T(8,128)(2,1)S(1)}, u32[]{:S(2)}, u32[]{:S(2)}) collective-permute-start(bf16[80,1024]{1,0:T(8,128)(2,1)S(1)} %get-tuple-element.30), channel_id=1, source_target_pairs={{0,1},{2,3},{4,5},{6,7},{8,9},{10,11},{12,13},{14,15},{16,17},{18,... | collective-permute-start | bytes 491528 | tf_op jit(solution)/shard_map/ppermute | solution.py:68
  6.4 0.7 collective-permute-start.1
  7.1 0.5 collective-permute-start.3
  7.5 0.8 collective-permute-done.3
  8.4 0.0 collective-permute-done.2.other
  8.4 0.0 copy-done
  8.4 0.0 copy-done.1
  8.4 10.2 %inner.1 = (f32[40,8192]{1,0:T(8,128)S(1)}, f32[40,8192]{1,0:T(8,128)S(1)}, f32[8192,128]{1,0:T(8,128)S(1)}, bf16[12,512,512]{2,1,0:T(8,128)(2,1)S(1)}, bf16[8,512,512]{2,1,0:T(8,128)(2,1)S(1)}) custom-call(f32[40,8192]{1,0:T(8,128)S(1)} %get-tuple-element.28.modes, f32[40,8192]{1,0:T(8,128)S(1)} %get-tuple-element.29.prev, ...), custom_call_target="tpu_custom_call" | custom-call | tf_op jit(solution)/shard_map/inner/pallas_call | solution.py:528
  18.6 0.0 collective-permute-done.near
  18.6 0.0 collective-permute-done.1.far
  18.6 4.0 %outer.1 = (f32[40,8192]{1,0:T(8,128)S(1)}, f32[40,8192]{1,0:T(8,128)S(1)}, f32[1,8192]{1,0:T(1,128)S(1)}, f32[128,128]{1,0:T(8,128)S(1)}) custom-call(f32[40,8192]{1,0:T(8,128)S(1)} %get-tuple-element.28.modes, f32[40,8192]{1,0:T(8,128)S(1)} %get-tuple-element.29.prev, bf16[80,1024]{1,0:T(8,128)(2,1)S(1)} %collective-permute-done.near, ...), custom_call_target="tpu_custom_call" | custom-call | tf_op jit(solution)/shard_map/outer/pallas_call | solution.py:545
  22.6 20.7 %all_to_all.28 = f32[128,1,128]{2,1,0:T(1,128)S(1)} all-to-all(f32[128,1,128]{2,1,0:T(1,128)S(1)} %bitcast.30), channel_id=1, replica_groups=mesh['field'=2,'dom_0'=4,'dom_1'=4,'dom_2'=4] {'field','dom_0','dom_1','..., dimensions={0} | all-to-all | bytes 131072 | tf_op jit(solution)/shard_map/all_to_all | solution.py:72
  43.3 0.3 residual.1
  43.7 0.8 collective-permute-start.6
  44.5 0.6 collective-permute-start.4
  45.0 0.8 collective-permute-start.5
  45.9 0.3 collective-permute-done.6.other
  46.2 8.1 %inner_second.1 = (f32[40,8192]{1,0:T(8,128)S(1)}, f32[8192,128]{1,0:T(8,128)S(1)}) custom-call(f32[8192,128]{1,0:T(8,128)S(1)} %get-tuple-element.37.coup.coupled, bf16[40,8192]{1,0:T(8,128)(2,1)S(1)} %get-tuple-element.44.whole, bf16[40,8192]{1,0:T(8,128)(2,1)S(1)} %collective-permute-done.6.other, ...), custom_call_target="tpu_custom_call", output_to_operand_aliasing={{1}: (0, {})} | custom-call | tf_op jit(solution)/shard_map/inner_second/pallas_call | solution.py:567
  54.3 0.0 collective-permute-done.4.near
  54.3 0.0 collective-permute-done.5.far
  54.3 6.3 %outer_second.1 = (f32[40,8192]{1,0:T(8,128)}, f32[128,128]{1,0:T(8,128)S(1)}) custom-call(f32[40,8192]{1,0:T(8,128)S(1)} %get-tuple-element.43.residual, bf16[40,8192]{1,0:T(8,128)(2,1)S(1)} %get-tuple-element.44.whole, bf16[40,1024]{1,0:T(8,128)(2,1)S(1)} %collective-permute-done.4.near, bf16[40,1024]{1,0:T(8,128)(2,1)S(1)} %collective-permute-done.5.far, ...), custom_call_target="tpu_custom_call" | custom-call | tf_op jit(solution)/shard_map/outer_second/pallas_call | solution.py:581
  60.6 18.1 %all_to_all.29 = f32[128,1,128]{2,1,0:T(1,128)S(1)} all-to-all(f32[128,1,128]{2,1,0:T(1,128)S(1)} %bitcast.29), channel_id=1, replica_groups=mesh['field'=2,'dom_0'=4,'dom_1'=4,'dom_2'=4] {'field','dom_0','dom_1','..., dimensions={0} | all-to-all | bytes 131072 | tf_op jit(solution)/shard_map/all_to_all | solution.py:72
  78.7 0.2 reduce_sum.9
  78.9 13.8 %all_to_all.30 = f32[128,1,128]{2,1,0:T(1,128)S(1)} all-to-all(f32[128,1,128]{2,1,0:T(1,128)S(1)} %broadcast_in_dim.4), channel_id=1, replica_groups=mesh['field'=2,'dom_0'=4,'dom_1'=4,'dom_2'=4] {'field','dom_0','dom_1','..., dimensions={0} | all-to-all | bytes 131072 | tf_op jit(solution)/shard_map/all_to_all | solution.py:72
  92.7 5.7 %final.1 = (f32[120,8192]{1,0:T(8,128)}, f32[120,120]{1,0:T(8,128)}) custom-call(f32[128,128]{1,0:T(8,128)S(1)} %bitcast.19, f32[40,8192]{1,0:T(8,128)S(1)} %get-tuple-element.28.modes, f32[40,8192]{1,0:T(8,128)} %get-tuple-element.51.residual_in, f32[40,8192]{1,0:T(8,128)S(1)} %get-tuple-element.29.prev), custom_call_target="tpu_custom_call" | custom-call | tf_op jit(solution)/shard_map/final/pallas_call | solution.py:602
  (1 shorter events, 0.0 us)
Async XLA Ops:
  1.3 7.1 %copy-start = (s32[1,3,1024]{2,0,1:T(1,128)S(1)}, s32[1,3,1024]{2,0,1:T(1,128)}, u32[]{:S(2)}) copy-start(s32[1,3,1024]{2,0,1:T(1,128)} %param.10) | copy-start | bytes 36868
  1.3 7.1 %copy-start.1 = (f32[1,3,1024]{2,0,1:T(1,128)S(1)}, f32[1,3,1024]{2,0,1:T(1,128)}, u32[]{:S(2)}) copy-start(f32[1,3,1024]{2,0,1:T(1,128)} %param.11) | copy-start | bytes 36868
  3.2 5.2 %collective-permute-start.2 = (bf16[80,8192]{1,0:T(8,128)(2,1)S(1)}, bf16[80,8192]{1,0:T(8,128)(2,1)S(1)}, u32[]{:S(2)}, u32[]{:S(2)}) collective-permute-start(bf16[80,8192]{1,0:T(8,128)(2,1)S(1)} %get-tuple-element.32), channel_id=1, source_target_pairs={{0,64},{64,0},{1,65},{65,1},{2,66},{66,2},{3,67},{67,3},{4,68},{68... | collective-permute-start | bytes 3932168 | tf_op jit(solution)/shard_map/ppermute | solution.py:55
  4.7 13.9 %collective-permute-start = (bf16[80,1024]{1,0:T(8,128)(2,1)S(1)}, bf16[80,1024]{1,0:T(8,128)(2,1)S(1)}, u32[]{:S(2)}, u32[]{:S(2)}) collective-permute-start(bf16[80,1024]{1,0:T(8,128)(2,1)S(1)} %get-tuple-element.30), channel_id=1, source_target_pairs={{0,1},{2,3},{4,5},{6,7},{8,9},{10,11},{12,13},{14,15},{16,17},{18,... | collective-permute-start | bytes 491528 | tf_op jit(solution)/shard_map/ppermute | solution.py:68
  6.4 12.1 %collective-permute-start.1 = (bf16[80,1024]{1,0:T(8,128)(2,1)S(1)}, bf16[80,1024]{1,0:T(8,128)(2,1)S(1)}, u32[]{:S(2)}, u32[]{:S(2)}) collective-permute-start(bf16[80,1024]{1,0:T(8,128)(2,1)S(1)} %get-tuple-element.31), channel_id=1, source_target_pairs={{1,2},{3,4},{5,6},{7,8},{9,10},{11,12},{13,14},{15,16},{17,18},{19... | collective-permute-start | bytes 491528 | tf_op jit(solution)/shard_map/ppermute | solution.py:68
  7.1 1.3 %collective-permute-start.3 = (s32[24,128]{1,0:T(8,128)S(1)}, s32[24,128]{1,0:T(8,128)S(1)}, u32[]{:S(2)}, u32[]{:S(2)}) collective-permute-start(s32[24,128]{1,0:T(8,128)S(1)} %get-tuple-element.33), channel_id=1, source_target_pairs={{0,64},{64,0},{1,65},{65,1},{2,66},{66,2},{3,67},{67,3},{4,68},{68... | collective-permute-start | bytes 36872 | tf_op jit(solution)/shard_map/ppermute | solution.py:55
  43.7 2.5 %collective-permute-start.6 = (bf16[40,8192]{1,0:T(8,128)(2,1)S(1)}, bf16[40,8192]{1,0:T(8,128)(2,1)S(1)}, u32[]{:S(2)}, u32[]{:S(2)}) collective-permute-start(bf16[40,8192]{1,0:T(8,128)(2,1)S(1)} %get-tuple-element.44.whole), channel_id=1, source_target_pairs={{0,64},{64,0},{1,65},{65,1},{2,66},{66,2},{3,67},{67,3},{4,68},{68... | collective-permute-start | bytes 1966088 | tf_op jit(solution)/shard_map/ppermute | solution.py:55
  44.5 9.8 %collective-permute-start.4 = (bf16[40,1024]{1,0:T(8,128)(2,1)S(1)}, bf16[40,1024]{1,0:T(8,128)(2,1)S(1)}, u32[]{:S(2)}, u32[]{:S(2)}) collective-permute-start(bf16[40,1024]{1,0:T(8,128)(2,1)S(1)} %get-tuple-element.45), channel_id=1, source_target_pairs={{0,1},{2,3},{4,5},{6,7},{8,9},{10,11},{12,13},{14,15},{16,17},{18,... | collective-permute-start | bytes 245768 | tf_op jit(solution)/shard_map/ppermute | solution.py:68
  45.0 9.2 %collective-permute-start.5 = (bf16[40,1024]{1,0:T(8,128)(2,1)S(1)}, bf16[40,1024]{1,0:T(8,128)(2,1)S(1)}, u32[]{:S(2)}, u32[]{:S(2)}) collective-permute-start(bf16[40,1024]{1,0:T(8,128)(2,1)S(1)} %get-tuple-element.46), channel_id=1, source_target_pairs={{1,2},{3,4},{5,6},{7,8},{9,10},{11,12},{13,14},{15,16},{17,18},{19... | collective-permute-start | bytes 245768 | tf_op jit(solution)/shard_map/ppermute | solution.py:68
